TPU v7x, 512 devices: a whole 4x8x8 slice. The times are simulated.
512 devices in a mesh: sta: 64 (over x, z, core), tpl: 8 (over y).
Axes of the slice: x: 4, y: 8, z: 8, core: 2. Of those that a mesh axis runs over, the one named last changes fastest.
Arguments:
- waveform: bfloat16 [64, 3, 6583], P('sta'), may hold values from -150 to 150
- templates: bfloat16 [512, 64, 1536], P('tpl', 'sta'), may hold values from -6 to 6
- lags: int32 [512, 64], P('tpl', 'sta'), may hold values from 0 to 3000
- present: int32 [512, 64], P('tpl', 'sta'), may hold values 0 or 1
Outputs:
- score: float32 [3072, 512], P('sta', 'tpl')
- scale_mad: float32 [512], P('tpl')
- peak: float32 [3072], P('sta')
All inputs are finite; a program needn't handle non-finite values. No bound on the sum of `present` on one device may be relied on, other than what follows from the above.
Results may differ from a plain program's by a relative error of at most 0.0003.
Values may be sent and summed in bfloat16 or wider, within the bound.
A program may use at most 64 MiB of HBM per device.

v0:
```python
import jax
import jax.numpy as jnp
from jax import lax
from jax.sharding import Mesh
from jax.sharding import PartitionSpec as P

LEN = 512
LAG = 3000
BINS = 1024
TOUT_DEV = 48
STA = ("sta_0", "sta_1", "sta_2")


def split_up(value, dim, devices):
    lengths = value.shape
    pieces = value.reshape(*lengths[:dim], devices, lengths[dim] // devices, *lengths[dim + 1 :])
    return jnp.moveaxis(pieces, dim, 0)


def joined_along(pieces, dim):
    pieces = jnp.moveaxis(pieces, 0, dim)
    lengths = pieces.shape
    return pieces.reshape(*lengths[:dim], lengths[dim] * lengths[dim + 1], *lengths[dim + 2 :])


def exchange_in_order(pieces, axes, turns):
    inside = pieces.shape[1:]
    out = pieces.reshape(*(lax.axis_size(a) for a in axes), *inside)
    for k in turns:
        out = lax.all_to_all(out, axes[k], k, k, tiled=True)
    return out.reshape(-1, *inside)


def exchange_by_chip(value, groups, turns, split_dim, concat_dim):
    devices = lax.axis_size(groups[0]) * lax.axis_size(groups[1])
    pieces = split_up(value, split_dim, devices)
    return joined_along(exchange_in_order(pieces, groups, turns), concat_dim)


def sent_and_summed(value, axis, dim):
    pieces = split_up(value, dim, lax.axis_size(axis))
    arrived = lax.all_to_all(pieces, axis, split_axis=0, concat_axis=0, tiled=True)
    return arrived.sum(axis=0)


def copy_for_each(value, axis):
    copies = jnp.broadcast_to(value, (lax.axis_size(axis), *value.shape))
    return lax.all_to_all(copies, axis, split_axis=0, concat_axis=0, tiled=True)


def gathered_copies(value, axis, dim):
    return joined_along(copy_for_each(value, axis), dim)


def of_everyone(value, axis):
    everything = copy_for_each(value, axis)
    return jnp.max(everything, axis=0)


def toeplitz_rows(record, length, columns):
    count = record.shape[1]
    chans = record.shape[0]
    tiled = jnp.broadcast_to(record[:, None, :], (chans, length + 1, count))
    tiled = tiled.reshape(chans, (length + 1) * count)[:, : length * (count + 1)]
    tiled = tiled.reshape(chans, length, count + 1)[:, :, :columns]
    return tiled.reshape(chans * length, columns)


def shift_rows(block, offsets, count):
    return jax.vmap(lambda row, offset: lax.dynamic_slice_in_dim(row, offset, count))(
        block, offsets
    )


def hat_counts(values, nbins):
    width = 512.0 / nbins
    ncols = values.shape[1]
    position = jnp.clip(jnp.abs(values) / width - 0.5, 0.0, nbins - 1.0)
    lower = jnp.minimum(jnp.floor(position), nbins - 2.0)
    weight = position - lower
    index = lower.astype(jnp.int32) + nbins * jnp.arange(ncols, dtype=jnp.int32)[None, :]
    flat_index = index.reshape(-1)
    flat_weight = weight.reshape(-1)
    counts = jax.ops.segment_sum(1.0 - flat_weight, flat_index, num_segments=ncols * nbins)
    counts = counts + jax.ops.segment_sum(flat_weight, flat_index + 1, num_segments=ncols * nbins)
    return counts.reshape(ncols, nbins)


def median_abs(counts, halfway):
    width = 512.0 / counts.shape[1]
    running = jnp.cumsum(counts, axis=1)
    earlier = running - counts
    share = jnp.clip((halfway - earlier) / jnp.maximum(counts, 1.0), 0.0, 1.0)
    return width * jnp.sum(share, axis=1)


def correlate_record(record, pattern, scaling, span):
    block_rows = 1024
    blocks = -(-span // block_rows)
    padded = jnp.pad(record, ((0, 0), (0, blocks * block_rows + LEN - record.shape[1])))

    def correlate(number, corr):
        begin = number * block_rows
        segment = lax.dynamic_slice_in_dim(padded, begin, block_rows + LEN, 1)
        columns = toeplitz_rows(segment, LEN, block_rows)
        result = jnp.dot(pattern, columns, preferred_element_type=jnp.float32) / scaling[:, None]
        return lax.dynamic_update_slice_in_dim(corr, result, begin, 1)

    return lax.fori_loop(
        0, blocks, correlate, jnp.zeros((pattern.shape[0], blocks * block_rows), jnp.float32)
    )


def on_device(waveform, templates, lags, present):
    stations = lax.axis_size(STA)
    total = TOUT_DEV * stations
    span = total + LAG
    record = waveform[0]
    pattern = templates[:, 0, :]
    offsets = lags[:, 0]
    member = present[:, 0].astype(jnp.float32)
    scaling = jnp.sqrt(jnp.sum(pattern.astype(jnp.float32) ** 2, axis=1) + 1e-06)
    corr = correlate_record(record, pattern, scaling, span)
    moved = shift_rows(corr, offsets, total) * member[:, None]
    arrived = exchange_by_chip(moved, (("sta_0", "sta_1"), "sta_2"), (1, 0), 1, 0)
    owned = jnp.sum(arrived.reshape(stations, moved.shape[0], TOUT_DEV), axis=0)
    stack = owned.T
    counts = hat_counts(stack, BINS)
    portion = sent_and_summed(counts, STA, 0)
    piece = median_abs(portion, 0.5 * total)
    median = gathered_copies(piece, STA, 0)
    scale_mad = 1.4826 * median
    score = stack / scale_mad[None, :]
    local_best = jnp.max(score, axis=1)
    peak = of_everyone(local_best, "tpl")
    return (score, scale_mad, peak)


def solution(mesh):
    torus = Mesh(
        mesh.devices.reshape(4, 8, 2, mesh.shape["tpl"]), ("sta_0", "sta_1", "sta_2", "tpl")
    )
    in_specs = (P(STA, None, None), P("tpl", STA, None), P("tpl", STA), P("tpl", STA))
    out_specs = (P(STA, "tpl"), P("tpl"), P(STA))
    return jax.shard_map(
        on_device, mesh=torus, in_specs=in_specs, out_specs=out_specs, check_vma=False
    )
```

profile of v0, /device:TPU:1, one launch (start us, length us, event | category | flops | bytes accessed | tf_op | source)
XLA Modules:
  0.0 505.1 jit_solution(15129122100957279783)
XLA Ops:
  2.8 210.3 %while.14 = (s32[]{:T(128)}, f32[64,6144]{1,0:T(8,128)S(1)}, bf16[3,6656]{1,0:T(4,128)(2,1)S(1)}, bf16[64,1536]{1,0:T(8,128)(2,1)S(1)}, f32[64]{0:T(128)S(1)}, /...) while((s32[]{:T(128)}, f32[64,6144]{1,0:T(8,128)S(1)}, bf16[3,6656]{1,0:T(4,128)(2,1)S(1)}, ...), condition=%wide.region_2.3_spmd, body=%wide.region_1.2_spmd.sunk | while | flops 201392128 | bytes 55583444 | solution.py:109
  2.8 2.5 broadcast_bitcast_fusion.2
  5.3 5.6 %copy.43 = bf16[1,3,513,1536]{3,1,2,0:T(4,128)(2,1)S(1)} copy(bf16[1,3,513,1536]{3,2,1,0:T(8,128)(2,1)} %broadcast_bitcast_fusion.2) | data formatting | bytes 9455616 | tf_op jit(solution)/shard_map/while
  10.9 3.8 slice.42
  14.7 9.1 %reshape.224 = bf16[2360832]{0:T(1024)(128)(2,1)} reshape(bf16[3,786944]{1,0:T(4,128)(2,1)} %slice.42) | data formatting | bytes 9443328 | tf_op jit(solution)/shard_map/while
  23.8 11.4 %reshape.225 = bf16[3,512,1537]{2,1,0:T(8,128)(2,1)} reshape(bf16[2360832]{0:T(1024)(128)(2,1)} %reshape.224) | data formatting | bytes 9443328 | tf_op jit(solution)/shard_map/while/body/eval_jaxpr/reshape | solution.py:65
  35.2 1.9 slice-done
  37.8 2.5 broadcast_bitcast_fusion.2
  40.3 5.6 %copy.43 = bf16[1,3,513,1536]{3,1,2,0:T(4,128)(2,1)S(1)} copy(bf16[1,3,513,1536]{3,2,1,0:T(8,128)(2,1)} %broadcast_bitcast_fusion.2) | data formatting | bytes 9455616 | tf_op jit(solution)/shard_map/while
  45.9 3.8 slice.42
  49.7 9.1 %reshape.224 = bf16[2360832]{0:T(1024)(128)(2,1)} reshape(bf16[3,786944]{1,0:T(4,128)(2,1)} %slice.42) | data formatting | bytes 9443328 | tf_op jit(solution)/shard_map/while
  58.8 11.4 %reshape.225 = bf16[3,512,1537]{2,1,0:T(8,128)(2,1)} reshape(bf16[2360832]{0:T(1024)(128)(2,1)} %reshape.224) | data formatting | bytes 9443328 | tf_op jit(solution)/shard_map/while/body/eval_jaxpr/reshape | solution.py:65
  70.2 1.9 slice-done
  72.8 2.5 broadcast_bitcast_fusion.2
  75.3 5.6 %copy.43 = bf16[1,3,513,1536]{3,1,2,0:T(4,128)(2,1)S(1)} copy(bf16[1,3,513,1536]{3,2,1,0:T(8,128)(2,1)} %broadcast_bitcast_fusion.2) | data formatting | bytes 9455616 | tf_op jit(solution)/shard_map/while
  80.9 3.8 slice.42
  84.7 9.1 %reshape.224 = bf16[2360832]{0:T(1024)(128)(2,1)} reshape(bf16[3,786944]{1,0:T(4,128)(2,1)} %slice.42) | data formatting | bytes 9443328 | tf_op jit(solution)/shard_map/while
  93.8 11.4 %reshape.225 = bf16[3,512,1537]{2,1,0:T(8,128)(2,1)} reshape(bf16[2360832]{0:T(1024)(128)(2,1)} %reshape.224) | data formatting | bytes 9443328 | tf_op jit(solution)/shard_map/while/body/eval_jaxpr/reshape | solution.py:65
  105.2 1.9 slice-done
  107.8 2.5 broadcast_bitcast_fusion.2
  110.3 5.6 %copy.43 = bf16[1,3,513,1536]{3,1,2,0:T(4,128)(2,1)S(1)} copy(bf16[1,3,513,1536]{3,2,1,0:T(8,128)(2,1)} %broadcast_bitcast_fusion.2) | data formatting | bytes 9455616 | tf_op jit(solution)/shard_map/while
  115.9 3.8 slice.42
  119.7 9.1 %reshape.224 = bf16[2360832]{0:T(1024)(128)(2,1)} reshape(bf16[3,786944]{1,0:T(4,128)(2,1)} %slice.42) | data formatting | bytes 9443328 | tf_op jit(solution)/shard_map/while
  128.9 11.4 %reshape.225 = bf16[3,512,1537]{2,1,0:T(8,128)(2,1)} reshape(bf16[2360832]{0:T(1024)(128)(2,1)} %reshape.224) | data formatting | bytes 9443328 | tf_op jit(solution)/shard_map/while/body/eval_jaxpr/reshape | solution.py:65
  140.3 1.9 slice-done
  142.9 2.5 broadcast_bitcast_fusion.2
  145.3 5.6 %copy.43 = bf16[1,3,513,1536]{3,1,2,0:T(4,128)(2,1)S(1)} copy(bf16[1,3,513,1536]{3,2,1,0:T(8,128)(2,1)} %broadcast_bitcast_fusion.2) | data formatting | bytes 9455616 | tf_op jit(solution)/shard_map/while
  150.9 3.8 slice.42
  154.8 9.1 %reshape.224 = bf16[2360832]{0:T(1024)(128)(2,1)} reshape(bf16[3,786944]{1,0:T(4,128)(2,1)} %slice.42) | data formatting | bytes 9443328 | tf_op jit(solution)/shard_map/while
  163.9 11.4 %reshape.225 = bf16[3,512,1537]{2,1,0:T(8,128)(2,1)} reshape(bf16[2360832]{0:T(1024)(128)(2,1)} %reshape.224) | data formatting | bytes 9443328 | tf_op jit(solution)/shard_map/while/body/eval_jaxpr/reshape | solution.py:65
  175.3 1.9 slice-done
  177.9 2.5 broadcast_bitcast_fusion.2
  180.3 5.6 %copy.43 = bf16[1,3,513,1536]{3,1,2,0:T(4,128)(2,1)S(1)} copy(bf16[1,3,513,1536]{3,2,1,0:T(8,128)(2,1)} %broadcast_bitcast_fusion.2) | data formatting | bytes 9455616 | tf_op jit(solution)/shard_map/while
  185.9 3.8 slice.42
  189.8 9.1 %reshape.224 = bf16[2360832]{0:T(1024)(128)(2,1)} reshape(bf16[3,786944]{1,0:T(4,128)(2,1)} %slice.42) | data formatting | bytes 9443328 | tf_op jit(solution)/shard_map/while
  198.9 11.4 %reshape.225 = bf16[3,512,1537]{2,1,0:T(8,128)(2,1)} reshape(bf16[2360832]{0:T(1024)(128)(2,1)} %reshape.224) | data formatting | bytes 9443328 | tf_op jit(solution)/shard_map/while/body/eval_jaxpr/reshape | solution.py:65
  210.3 1.9 slice-done
  213.1 147.9 %while.15 = (s32[]{:T(128)}, f32[64,6144]{1,0:T(8,128)S(1)}, s32[64,2]{0,1:T(2,128)S(1)}, f32[64,3072]{1,0:T(8,128)S(1)}, s32[]{:T(128)}, /*index=5*/s32[]{:T(128)}) while((s32[]{:T(128)}, f32[64,6144]{1,0:T(8,128)S(1)}, s32[64,2]{0,1:T(2,128)S(1)}, f32[64,3072]{1,0:T(8,128)S(1)}, s32[]{:T(128)}, /*index=5*/s32[]{:T(128)}) %tuple.55), condition=%wide.while_cond, body=%wide.while_body.sunk | while | flops 2 | bytes 49273 | solution.py:70
  213.7 1.4 dynamic-slice.7
  218.3 1.4 dynamic-slice.7
  220.6 1.4 dynamic-slice.7
  222.9 1.4 dynamic-slice.7
  225.3 1.4 dynamic-slice.7
  227.6 1.4 dynamic-slice.7
  229.9 1.4 dynamic-slice.7
  232.2 1.4 dynamic-slice.7
  236.8 1.4 dynamic-slice.7
  239.1 1.4 dynamic-slice.7
  361.0 2.3 gather.6
  363.3 1.8 broadcast_multiply_fusion
  365.1 2.4 copy.31
  367.4 2.1 reshape.218
  369.6 10.8 %all_to_all.27 = f32[2,1,98304]{2,1,0:T(1,128)S(1)} all-to-all(f32[2,1,98304]{2,1,0:T(1,128)S(1)} %reshape.218), channel_id=1, replica_groups=mesh['sta_0'=4,'sta_1'=8,'sta_2'=2,'tpl'=8] {'sta_2'}, dimensions={0} | all-to-all | bytes 1572864 | tf_op jit(solution)/shard_map/all_to_all | solution.py:30
  380.9 3.1 reduce.13
  385.2 1.9 reshape.220
  387.0 7.5 %all-to-all-start.1 = ((f32[32,1,6144]{2,1,0:T(1,128)}), f32[32,1,6144]{2,1,0:T(1,128)S(1)}, u32[]{:S(2)}, u32[]{:S(2)}) async-start(f32[32,1,6144]{2,1,0:T(1,128)} %reshape.220), calls=%async_computation.1 | async-start | bytes 1572864 | tf_op jit(solution)/shard_map/all_to_all | solution.py:30
  394.6 18.8 %all-to-all-done.1 = f32[32,1,6144]{2,1,0:T(1,128)S(1)} async-done(((f32[32,1,6144]{2,1,0:T(1,128)}), f32[32,1,6144]{2,1,0:T(1,128)S(1)}, u32[]{:S(2)}, u32[]{:S(2)}) %all-to-all-start.1) | async-done | bytes 786464 | tf_op jit(solution)/shard_map/all_to_all | solution.py:30
  413.4 2.5 reduce.14
  416.9 32.6 %scatter_custom_fusion = f32[65536]{0:T(1024)S(1)} fusion(s32[6144]{0:T(1024)S(1)} %bitcast.85, f32[6144]{0:T(1024)S(1)} %pad_maximum_fusion, f32[]{:T(128)} %constant.61.clone.1), kind=kCustom, calls=%fused_computation.9 | custom fusion | flops 6144 | bytes 262148 | tf_op jit(solution)/shard_map/add | solution.py:85
  449.6 22.2 %all_to_all.28 = f32[64,1,1024]{2,1,0:T(1,128)S(1)} all-to-all(f32[64,1,1024]{2,1,0:T(1,128)S(1)} %bitcast.82), channel_id=1, replica_groups=mesh['sta_0'=4,'sta_1'=8,'sta_2'=2,'tpl'=8] {'sta_0','sta_1','sta_2'}, dimensions={0} | all-to-all | bytes 524288 | tf_op jit(solution)/shard_map/all_to_all | solution.py:42
  474.5 6.0 %all-to-all-start.3 = ((f32[64,1,1]{2,1,0:T(1,128)}), f32[64,1,1]{2,1,0:T(1,128)S(1)}, u32[]{:S(2)}, u32[]{:S(2)}) async-start(f32[64,1,1]{2,1,0:T(1,128)} %broadcast_in_dim.34), calls=%async_computation.3 | async-start | bytes 65536 | tf_op jit(solution)/shard_map/all_to_all | solution.py:48
  480.7 9.2 %all-to-all-done.3 = f32[64,1,1]{2,1,0:T(1,128)S(1)} async-done(((f32[64,1,1]{2,1,0:T(1,128)}), f32[64,1,1]{2,1,0:T(1,128)S(1)}, u32[]{:S(2)}, u32[]{:S(2)}) %all-to-all-start.3) | async-done | bytes 288 | tf_op jit(solution)/shard_map/all_to_all | solution.py:48
  491.2 6.8 %all-to-all-start.4 = ((f32[8,1,48]{2,1,0:T(1,128)}), f32[8,1,48]{2,1,0:T(1,128)S(1)}, u32[]{:S(2)}, u32[]{:S(2)}) async-start(f32[8,1,48]{2,1,0:T(1,128)} %broadcast_in_dim.35), calls=%async_computation.4 | async-start | bytes 8192 | tf_op jit(solution)/shard_map/all_to_all | solution.py:48
  498.7 5.9 %all-to-all-done.4 = f32[8,1,48]{2,1,0:T(1,128)S(1)} async-done(((f32[8,1,48]{2,1,0:T(1,128)}), f32[8,1,48]{2,1,0:T(1,128)S(1)}, u32[]{:S(2)}, u32[]{:S(2)}) %all-to-all-start.4) | async-done | bytes 1568 | tf_op jit(solution)/shard_map/all_to_all | solution.py:48
  (309 shorter events, 145.5 us)
Async XLA Ops:
  0.6 2.1 copy-start
  2.8 210.3 %copy-start.2 = (s32[64,1]{0,1:T(1,128)S(1)}, s32[64,1]{0,1:T(1,128)}, u32[]{:S(2)}) copy-start(s32[64,1]{0,1:T(1,128)} %param.8) | copy-start | bytes 772
  35.2 1.9 slice-start
  70.2 1.9 slice-start
  105.2 1.9 slice-start
  140.3 1.9 slice-start
  175.3 1.9 slice-start
  210.3 1.9 slice-start
  213.1 150.2 %copy-start.3 = (s32[64,1]{0,1:T(1,128)S(1)}, s32[64,1]{0,1:T(1,128)}, u32[]{:S(2)}) copy-start(s32[64,1]{0,1:T(1,128)} %param.9) | copy-start | bytes 772
  387.0 26.4 %all-to-all-start.1 = ((f32[32,1,6144]{2,1,0:T(1,128)}), f32[32,1,6144]{2,1,0:T(1,128)S(1)}, u32[]{:S(2)}, u32[]{:S(2)}) async-start(f32[32,1,6144]{2,1,0:T(1,128)} %reshape.220), calls=%async_computation.1 | async-start | bytes 1572864 | tf_op jit(solution)/shard_map/all_to_all | solution.py:30
  474.5 15.4 %all-to-all-start.3 = ((f32[64,1,1]{2,1,0:T(1,128)}), f32[64,1,1]{2,1,0:T(1,128)S(1)}, u32[]{:S(2)}, u32[]{:S(2)}) async-start(f32[64,1,1]{2,1,0:T(1,128)} %broadcast_in_dim.34), calls=%async_computation.3 | async-start | bytes 65536 | tf_op jit(solution)/shard_map/all_to_all | solution.py:48
  490.4 14.6 %copy-start.1 = (f32[64]{0:T(128)}, f32[64]{0:T(128)S(1)}, u32[]{:S(2)}) copy-start(f32[64]{0:T(128)S(1)} %multiply_reduce_fusion.1) | copy-start | bytes 772
  491.2 13.4 %all-to-all-start.4 = ((f32[8,1,48]{2,1,0:T(1,128)}), f32[8,1,48]{2,1,0:T(1,128)S(1)}, u32[]{:S(2)}, u32[]{:S(2)}) async-start(f32[8,1,48]{2,1,0:T(1,128)} %broadcast_in_dim.35), calls=%async_computation.4 | async-start | bytes 8192 | tf_op jit(solution)/shard_map/all_to_all | solution.py:48
where the time goes:
time: 507 us; the launch traced here: 505 us
  local copies, waits for them, and re-layouts  366 us (72%)
  other arithmetic  43.9 us (9%)
  waiting for transfers between devices  33.9 us (7%)
  blocking collectives  33 us (7%)
  starting transfers between devices  20.4 us (4%)
    gather x256, local copies, waits for them, and re-layouts  146 us
    while x18, local copies, waits for them, and re-layouts  103 us
    reshape x6, local copies, waits for them, and re-layouts, toeplitz_rows(): tiled = tiled.reshape(chans, length, count + 1)[:, :, :columns]  68.4 us
    add x1, other arithmetic, hat_counts(): counts + jax.ops.segment_sum(flat_weight, flat_index + 1, num_segments=nc...  32.6 us
    slice x6, local copies, waits for them, and re-layouts, toeplitz_rows(): tiled = tiled.reshape(chans, (length + 1) * count)[:, :length * (count + 1)]  23 us
    all_to_all x1, blocking collectives, sent_and_summed(): lax.all_to_all(pieces, axis, split_axis=0, concat_axis=0, tiled=True)  22.2 us
    all_to_all x1, waiting for transfers between devices, exchange_in_order(): out = lax.all_to_all(out, axes[k], k, k, tiled=True)  18.8 us
    all_to_all x2, waiting for transfers between devices, copy_for_each(): return lax.all_to_all(copies, axis, split_axis=0, concat_axis=0, tiled=True)  15.1 us
  transfers between devices with their start and end apart: 3, of which 3 were waited for; matrix products, arithmetic and copies ran while one was open for 0% of the time, Pallas kernels for 0%

commit v1 on v0

v1 whole, which is shorter than its diff:
```python
import functools

import jax
import jax.numpy as jnp
from jax import lax
from jax.experimental import pallas as pl
from jax.experimental.pallas import tpu as pltpu
from jax.sharding import PartitionSpec as P

LEN = 512
CHANS = 3
SAMPLES = 6583
BINS = 1024
TOUT = 3072
NT = 64
TAPS = 128
NQ = LEN // TAPS
NBLK = 52
CH = 4
ROWS = TOUT // 128
OWN = TOUT // 64
F32 = jnp.float32
BF16 = jnp.bfloat16
MESH = pl.DeviceIdType.MESH


def kernel(
    wave_ref, temp_ref, lag_ref, pres_ref, score_ref, mad_ref, peak_ref,
    wrow, amat, hank, part, scl, sendc, own, recvc, sendx, recvx, sendz, recvz,
    outr, got, pk, pkgot,
    sem_cs, sem_cr, sem_xs, sem_xr, sem_zs, sem_zr, sem_os, sem_or, sem_ps, sem_pr,
):
    s = lax.axis_index("sta")
    tp = lax.axis_index("tpl")
    x, z, c = s // 16, (s // 2) % 8, s % 2

    def dev(xx, zz, cc):
        return (xx * 16 + zz * 2 + cc, tp)

    barrier = pltpu.get_barrier_semaphore()

    def greet(i, _):
        pl.semaphore_signal(barrier, inc=1, device_id=((s + i) % 64, tp), device_id_type=MESH)
        return 0

    lax.fori_loop(1, 64, greet, 0)

    def greet_tpl(i, _):
        pl.semaphore_signal(barrier, inc=1, device_id=(s, (tp + i) % 8), device_id_type=MESH)
        return 0

    lax.fori_loop(1, 8, greet_tpl, 0)

    wrow[...] = jnp.zeros(wrow.shape, F32)
    wrow[0:CHANS, 0:SAMPLES] = wave_ref[...].astype(F32)

    total = jnp.zeros((NT, 128), F32)
    flip_i = lax.broadcasted_iota(jnp.int32, (128, 128), 0)
    flip_j = lax.broadcasted_iota(jnp.int32, (128, 128), 1)
    flip = jnp.where(flip_i + flip_j == 127, 1.0, 0.0).astype(BF16)
    for ch in range(CHANS):
        for q in range(NQ):
            piece = temp_ref[:, (ch * NQ + q) * 128 : (ch * NQ + q + 1) * 128]
            wide = piece.astype(F32)
            total = total + wide * wide
            turned = jnp.dot(piece, flip, preferred_element_type=F32).astype(BF16)
            amat[q * NT : (q + 1) * NT, ch * 128 : (ch + 1) * 128] = turned
    norm = jnp.sqrt(jnp.sum(total, axis=1, keepdims=True) + 1e-6)
    scl[...] = jnp.broadcast_to(1.0 / norm, (NT, 128))

    rho = lax.broadcasted_iota(jnp.int32, (128, 128), 0)
    lane = lax.broadcasted_iota(jnp.int32, (128, 128), 1)
    first = lane <= rho

    def chunk(j, _):
        for ch in range(CHANS):
            turned = []
            for b in range(CH + 1):
                at = pl.multiple_of((j * CH + b) * 128, 128)
                row = wrow[ch : ch + 1, pl.ds(at, 128)]
                turned.append(
                    pltpu.roll(jnp.broadcast_to(row, (128, 128)), 1, 1, stride=1, stride_axis=0)
                )
            for b in range(CH):
                block = jnp.where(first, turned[b], turned[b + 1])
                hank[ch * 128 : (ch + 1) * 128, b * 128 : (b + 1) * 128] = block.astype(BF16)
        out = jnp.dot(amat[...], hank[...], preferred_element_type=F32)
        for g in range(NQ * NT // 8):
            for b in range(CH):
                part[pl.ds(g * 8 * NBLK + j * CH + b, 8, stride=NBLK), :] = out[
                    g * 8 : (g + 1) * 8, b * 128 : (b + 1) * 128
                ]
        return 0

    lax.fori_loop(0, NBLK // CH, chunk, 0)

    lane24 = lax.broadcasted_iota(jnp.int32, (ROWS, 128), 1)

    def shifted(t):
        lag = lag_ref[0, t]
        here = pres_ref[0, t].astype(F32)
        a, r = lag // 128, lag % 128
        left = right = None
        for q in range(NQ):
            at = (q * NT + t) * NBLK + q + a
            one, two = part[pl.ds(at, ROWS), :], part[pl.ds(at + 1, ROWS), :]
            left = one if left is None else left + one
            right = two if right is None else right + two
        by = (128 - r) % 128
        left, right = pltpu.roll(left, by, 1), pltpu.roll(right, by, 1)
        return jnp.where(lane24 < 128 - r, left, right) * (scl[pl.ds(t, 1), :] * here)

    def copy_c(d):
        return pltpu.make_async_remote_copy(
            src_ref=sendc.at[d], dst_ref=recvc.at[d], send_sem=sem_cs.at[d], recv_sem=sem_cr.at[d],
            device_id=dev(x, z, 1 - c), device_id_type=MESH)

    def copy_x(d):
        return pltpu.make_async_remote_copy(
            src_ref=sendx.at[d - 1], dst_ref=recvx.at[d - 1], send_sem=sem_xs.at[d - 1],
            recv_sem=sem_xr.at[d - 1], device_id=dev((x + d) % 4, z, c), device_id_type=MESH)

    def copy_z(d):
        return pltpu.make_async_remote_copy(
            src_ref=sendz.at[d - 1], dst_ref=recvz.at[d - 1], send_sem=sem_zs.at[d - 1],
            recv_sem=sem_zr.at[d - 1], device_id=dev(x, (z + d) % 8, c), device_id_type=MESH)

    def fold(d):
        copy_c(d).wait_recv()
        if d > 0:
            sendx[d - 1] = own[d] + recvc[d]
            copy_x(d).start()

    previous = None
    for d in (2, 1, 3, 0):
        base = ((x + d) % 4) * 16

        def theirs(i, _):
            for k in range(4):
                zz = i * 4 + k
                sendc[d, zz] = shifted(base + zz * 2 + 1 - c)
            return 0

        def ours(i, _):
            for k in range(4):
                zz = i * 4 + k
                own[d, zz] = shifted(base + zz * 2 + c)
            return 0

        lax.fori_loop(0, 2, theirs, 0)
        if previous is None:
            pl.semaphore_wait(barrier, 63 + 7)
        copy_c(d).start()
        lax.fori_loop(0, 2, ours, 0)
        if previous is not None:
            fold(previous)
        previous = d
    fold(0)
    for d in (1, 3, 2):
        copy_x(d).wait_recv()

    def reduced(zz):
        return (own[0, zz] + recvc[0, zz]) + (recvx[0, zz] + recvx[1, zz] + recvx[2, zz])

    for d in (4, 3, 5, 2, 6, 1, 7):
        sendz[d - 1] = reduced((z + d) % 8)
        copy_z(d).start()
    row = reduced(z)
    for d in (1, 7, 2, 6, 3, 5, 4):
        copy_z(d).wait_recv()
        row = row + recvz[d - 1]

    pos = jnp.clip(jnp.abs(row) * (BINS / 512.0) - 0.5, 0.0, BINS - 1.0)
    low = jnp.minimum(jnp.floor(pos), BINS - 2.0)
    high = jnp.floor(low * (1.0 / 32.0))
    inside = pos - 32.0 * high
    iota_h = lax.broadcasted_iota(jnp.int32, (32, 128), 0).astype(F32)
    iota_l = lax.broadcasted_iota(jnp.int32, (40, 128), 0).astype(F32)
    ones, hats = [], [[], [], []]
    for i in range(ROWS):
        ones.append(jnp.where(iota_h == high[i : i + 1, :], 1.0, 0.0).astype(BF16))
        hat = jnp.maximum(1.0 - jnp.abs(inside[i : i + 1, :] - iota_l), 0.0)
        for k in range(3):
            near = hat.astype(BF16)
            hats[k].append(near)
            hat = hat - near.astype(F32)
    ones = jnp.concatenate(ones, axis=1)
    counts = None
    for k in range(3):
        got_k = lax.dot_general(
            jnp.concatenate(hats[k], axis=1), ones, (((1,), (1,)), ((), ())),
            preferred_element_type=F32)
        counts = got_k if counts is None else counts + got_k
    over = jnp.concatenate([jnp.zeros((1, 1), F32), counts[32:33, 0:31]], axis=1)
    row_l = lax.broadcasted_iota(jnp.int32, (32, 32), 0)
    col_h = lax.broadcasted_iota(jnp.int32, (32, 32), 1)
    counts = counts[0:32, :] + jnp.where(row_l == 0, jnp.broadcast_to(over, (32, 32)), 0.0)
    below = jnp.where(col_h < row_l, 1.0, 0.0)
    above = jnp.where(row_l < col_h, 1.0, 0.0)
    sums = jnp.broadcast_to(jnp.sum(counts, axis=0, keepdims=True), (8, 32))
    before = jnp.dot(below, counts, precision=lax.Precision.HIGHEST, preferred_element_type=F32)
    before = before + jnp.dot(
        sums, above, precision=lax.Precision.HIGHEST, preferred_element_type=F32)[0:1, :]
    share = jnp.clip((0.5 * TOUT - before) / jnp.maximum(counts, 1.0), 0.0, 1.0)
    share = jnp.sum(jnp.sum(share, axis=1, keepdims=True), axis=0, keepdims=True)
    mad = 1.4826 * ((512.0 / BINS) * share)
    pk[...] = row / mad
    madrow = jnp.broadcast_to(mad, (8, 128))

    lane8 = lax.broadcasted_iota(jnp.int32, (8, 128), 1)
    for j in range(8):
        at, off = (OWN * j) // 128, (OWN * j) % 128
        piece = pk[pl.ds(at, 8, stride=3), :]
        if off:
            piece = pltpu.roll(piece, 128 - off, 1)
            if off + OWN > 128:
                nxt = pltpu.roll(pk[pl.ds(at + 1, 8, stride=3), :], 128 - off, 1)
                piece = jnp.where(lane8 < 128 - off, piece, nxt)
        piece = jnp.where(lane8 < OWN, piece, madrow)
        for g in range(8):
            outr[8 * g + j] = piece[g : g + 1, :]

    def copy_o(i):
        to = (s + i) % 64
        return pltpu.make_async_remote_copy(
            src_ref=outr.at[to], dst_ref=got.at[s], send_sem=sem_os, recv_sem=sem_or,
            device_id=(to, tp), device_id_type=MESH)

    def send(i, _):
        copy_o((i + 32) % 64).start()
        return 0

    lax.fori_loop(0, 32, send, 0)
    lax.fori_loop(33, 64, send, 0)
    got[s] = outr[s]
    pltpu.make_async_copy(outr.at[pl.ds(0, 63)], got.at[pl.ds(0, 63)], sem_or).wait()

    best = jnp.max(got[...], axis=0)
    pkgot[0] = best

    def copy_p(d):
        return pltpu.make_async_remote_copy(
            src_ref=pkgot.at[0], dst_ref=pkgot.at[d], send_sem=sem_ps.at[d - 1],
            recv_sem=sem_pr.at[d - 1], device_id=(s, (tp + d) % 8), device_id_type=MESH)

    for d in (4, 3, 5, 2, 6, 1, 7):
        copy_p(d).start()
    flat = jnp.concatenate([got[i] for i in range(64)] + [jnp.zeros((64, 128), F32)], axis=0)
    turned = flat.T
    score_ref[...] = turned[0:OWN, 0:NT]
    mad_ref[...] = turned[OWN : OWN + 1, 0:NT]
    for d in (1, 7, 2, 6, 3, 5, 4):
        copy_p(d).wait_recv()
        best = jnp.maximum(best, pkgot[d])
    peak_ref[...] = best[:, 0:OWN]

    for d in range(4):
        copy_c(d).wait_send()
    for d in range(1, 4):
        copy_x(d).wait_send()
    for d in range(1, 8):
        copy_z(d).wait_send()
        copy_p(d).wait_send()
    pltpu.make_async_copy(outr.at[pl.ds(0, 63)], got.at[pl.ds(0, 63)], sem_os).wait()


def on_device(waveform, templates, lags, present):
    vmem = pl.BlockSpec(memory_space=pltpu.VMEM)
    smem = pl.BlockSpec(memory_space=pltpu.SMEM)
    dma = pltpu.SemaphoreType.DMA
    score, mad, peak = pl.pallas_call(
        kernel,
        out_shape=(
            jax.ShapeDtypeStruct((OWN, NT), F32),
            jax.ShapeDtypeStruct((1, NT), F32),
            jax.ShapeDtypeStruct((1, OWN), F32),
        ),
        in_specs=[vmem, vmem, smem, smem],
        out_specs=(vmem, vmem, vmem),
        scratch_shapes=[
            pltpu.VMEM((8, (NBLK + 1) * 128), F32),
            pltpu.VMEM((NQ * NT, CHANS * TAPS), BF16),
            pltpu.VMEM((CHANS * TAPS, CH * 128), BF16),
            pltpu.VMEM((NQ * NT * NBLK, 128), F32),
            pltpu.VMEM((NT, 128), F32),
            pltpu.VMEM((4, 8, ROWS, 128), F32),
            pltpu.VMEM((4, 8, ROWS, 128), F32),
            pltpu.VMEM((4, 8, ROWS, 128), F32),
            pltpu.VMEM((3, 8, ROWS, 128), F32),
            pltpu.VMEM((3, 8, ROWS, 128), F32),
            pltpu.VMEM((7, ROWS, 128), F32),
            pltpu.VMEM((7, ROWS, 128), F32),
            pltpu.VMEM((64, 1, 128), F32),
            pltpu.VMEM((64, 1, 128), F32),
            pltpu.VMEM((ROWS, 128), F32),
            pltpu.VMEM((8, 1, 128), F32),
            dma((4,)), dma((4,)), dma((3,)), dma((3,)), dma((7,)), dma((7,)),
            dma(()), dma(()), dma((7,)), dma((7,)),
        ],
        compiler_params=pltpu.CompilerParams(
            collective_id=0, has_side_effects=True, vmem_limit_bytes=50 * 1024 * 1024),
    )(waveform[0], templates[:, 0, :], lags.reshape(1, NT), present.reshape(1, NT))
    return score, mad[0], peak[0]


def solution(mesh):
    return jax.shard_map(
        on_device,
        mesh=mesh,
        in_specs=(P("sta", None, None), P("tpl", "sta", None), P("tpl", "sta"), P("tpl", "sta")),
        out_specs=(P("sta", "tpl"), P("tpl"), P("sta")),
        check_vma=False,
    )
```

time: 507 us -> 49.5 us (0.10)
  local copies, waits for them, and re-layouts: 366 us -> 4.02 us
  Pallas kernels: 0 us -> 44.6 us
  other arithmetic: 43.9 us -> 0 us
  waiting for transfers between devices: 33.9 us -> 0 us
  blocking collectives: 33 us -> 0 us
  starting transfers between devices: 20.4 us -> 0 us
    gather x257 -> x0, local copies, waits for them, and re-layouts: 148 us -> none
    while x18 -> x0, local copies, waits for them, and re-layouts: 103 us -> none
    reshape x8 -> x0, local copies, waits for them, and re-layouts: 70.8 us -> none  [the longest x6 68.4 us: toeplitz_rows(): tiled = tiled.reshape(chans, length, count + 1)[:, :, :columns]]
    pallas_call x0 -> x1, Pallas kernels: none -> 44.6 us  [on_device(): pl.pallas_call(kernel, out_shape=(jax.ShapeDtypeStruct((OWN, NT), F32), j...]
    slice x18 -> x0, local copies, waits for them, and re-layouts: 34.4 us -> none  [the longest x6 23 us: toeplitz_rows(): tiled = tiled.reshape(chans, (length + 1) * count)[:, :length * (count + 1)]]
    all_to_all x3 -> x0, waiting for transfers between devices: 33.9 us -> none  [the longest x1 18.8 us: exchange_in_order(): out = lax.all_to_all(out, axes[k], k, k, tiled=True)]
    all_to_all x2 -> x0, blocking collectives: 33 us -> none  [the longest x1 22.2 us: sent_and_summed(): lax.all_to_all(pieces, axis, split_axis=0, concat_axis=0, tiled=True)]
    add x3 -> x0, other arithmetic: 32.6 us -> none  [the longest x1 32.6 us: hat_counts(): counts + jax.ops.segment_sum(flat_weight, flat_index + 1, num_segments=nc...]
  transfers between devices with their start and end apart: 3 -> 0, of which waited for: 3 -> 0; matrix products, arithmetic and copies ran while one was open for 0% -> 0% of each run, Pallas kernels for 0% -> 0%
where the time goes in v1:
time: 49.5 us; the launch traced here: 49.3 us
  Pallas kernels  44.6 us (90%)
  local copies, waits for them, and re-layouts  4.02 us (8%)
  between operations  0.66 us (1%)
    pallas_call x1, Pallas kernels, on_device(): pl.pallas_call(kernel, out_shape=(jax.ShapeDtypeStruct((OWN, NT), F32), j...  44.6 us
    unnamed x11, local copies, waits for them, and re-layouts  4.02 us

profile of v1, /device:TPU:1, one launch (start us, length us, event | category | flops | bytes accessed | tf_op | source)
XLA Modules:
  0.0 49.3 jit_solution(17361761298072187596)
XLA Ops:
  0.6 0.0 copy-start.2
  0.6 0.0 copy-start.3
  0.7 0.6 %copy-done.2 = s32[64,1]{0,1:T(1,128)S(1)} copy-done((s32[64,1]{0,1:T(1,128)S(1)}, s32[64,1]{0,1:T(1,128)}, u32[]{:S(2)}) %copy-start.2) | copy-done | bytes 280
  1.3 0.0 copy-done.3
  1.3 0.0 copy-start
  1.3 0.9 %copy-done = bf16[64,1,1536]{2,0,1:T(8,128)(2,1)S(1)} copy-done((bf16[64,1,1536]{2,0,1:T(8,128)(2,1)S(1)}, bf16[64,1,1536]{2,0,1:T(8,128)(2,1)}, u32[]{:S(2)}) %copy-start) | copy-done | bytes 196632
  2.2 0.0 copy-start.1
  2.2 0.8 %copy-done.1 = bf16[1,3,6583]{2,1,0:T(4,128)(2,1)S(1)} copy-done((bf16[1,3,6583]{2,1,0:T(4,128)(2,1)S(1)}, bf16[1,3,6583]{2,1,0:T(4,128)(2,1)}, u32[]{:S(2)}) %copy-start.1) | copy-done | bytes 39522
  3.0 44.6 %shard_map.67 = (f32[48,64]{1,0:T(8,128)S(1)}, f32[1,64]{1,0:T(1,128)S(1)}, f32[1,48]{1,0:T(1,128)S(1)}) custom-call(bf16[3,6583]{1,0:T(4,128)(2,1)S(1)} %bitcast.7, bf16[64,1536]{1,0:T(8,128)(2,1)S(1)} %bitcast.6, s32[1,64]{1,0:T(1,128)S(1)} %bitcast.8, s32[1,64]{1,0:T(1,128)S(1)} %bitcast.9), custom_call_target="tpu_custom_call" | custom-call | tf_op jit(solution)/shard_map/pallas_call | solution.py:271
  47.6 0.6 %copy.10 = f32[48,64]{1,0:T(8,128)} copy(f32[48,64]{1,0:T(8,128)S(1)} %get-tuple-element.12) | data formatting | bytes 24576
  48.3 0.5 %copy.11 = f32[64]{0:T(128)} copy(f32[64]{0:T(128)S(1)} %bitcast.11) | data formatting | bytes 512
  48.8 0.5 %copy.12 = f32[48]{0:T(128)} copy(f32[48]{0:T(128)S(1)} %bitcast.10) | data formatting | bytes 384
Async XLA Ops:
  0.6 0.7 %copy-start.2 = (s32[64,1]{0,1:T(1,128)S(1)}, s32[64,1]{0,1:T(1,128)}, u32[]{:S(2)}) copy-start(s32[64,1]{0,1:T(1,128)} %param.6) | copy-start | bytes 772
  0.6 0.7 %copy-start.3 = (s32[64,1]{0,1:T(1,128)S(1)}, s32[64,1]{0,1:T(1,128)}, u32[]{:S(2)}) copy-start(s32[64,1]{0,1:T(1,128)} %param.7) | copy-start | bytes 772
  1.3 0.9 %copy-start = (bf16[64,1,1536]{2,0,1:T(8,128)(2,1)S(1)}, bf16[64,1,1536]{2,0,1:T(8,128)(2,1)}, u32[]{:S(2)}) copy-start(bf16[64,1,1536]{2,0,1:T(8,128)(2,1)} %param.5) | copy-start | bytes 589828
  2.2 0.8 %copy-start.1 = (bf16[1,3,6583]{2,1,0:T(4,128)(2,1)S(1)}, bf16[1,3,6583]{2,1,0:T(4,128)(2,1)}, u32[]{:S(2)}) copy-start(bf16[1,3,6583]{2,1,0:T(4,128)(2,1)} %param.4) | copy-start | bytes 118498

commit v2 on v1

--- a/solution.py
+++ b/solution.py
@@ -25,8 +25,8 @@
 
 
 def kernel(
-    wave_ref, temp_ref, lag_ref, pres_ref, score_ref, mad_ref, peak_ref,
-    wrow, amat, hank, part, scl, sendc, own, recvc, sendx, recvx, sendz, recvz,
+    wave_hbm, temp_hbm, lag_hbm, pres_hbm, score_ref, mad_ref, peak_ref,
+    wave_ref, temp_ref, lag_ref, pres_ref, sem_in, wrow, amat, hank, hank2, part, scl, sendc, own, recvc, sendx, recvx, sendz, recvz,
     outr, got, pk, pkgot,
     sem_cs, sem_cr, sem_xs, sem_xr, sem_zs, sem_zr, sem_os, sem_or, sem_ps, sem_pr,
 ):
@@ -37,21 +37,25 @@
     def dev(xx, zz, cc):
         return (xx * 16 + zz * 2 + cc, tp)
 
+    inputs = [
+        pltpu.make_async_copy(a, b, sem_in.at[i])
+        for i, (a, b) in enumerate(
+            ((temp_hbm, temp_ref), (wave_hbm, wave_ref), (lag_hbm, lag_ref), (pres_hbm, pres_ref))
+        )
+    ]
+    for copy in inputs:
+        copy.start()
+
     barrier = pltpu.get_barrier_semaphore()
-
-    def greet(i, _):
+    for i in range(1, 8):
+        pl.semaphore_signal(barrier, inc=1, device_id=(s, (tp + i) % 8), device_id_type=MESH)
+
+    def greet(i):
         pl.semaphore_signal(barrier, inc=1, device_id=((s + i) % 64, tp), device_id_type=MESH)
-        return 0
-
-    lax.fori_loop(1, 64, greet, 0)
-
-    def greet_tpl(i, _):
-        pl.semaphore_signal(barrier, inc=1, device_id=(s, (tp + i) % 8), device_id_type=MESH)
-        return 0
-
-    lax.fori_loop(1, 8, greet_tpl, 0)
 
     wrow[...] = jnp.zeros(wrow.shape, F32)
+    for copy in inputs:
+        copy.wait()
     wrow[0:CHANS, 0:SAMPLES] = wave_ref[...].astype(F32)
 
     total = jnp.zeros((NT, 128), F32)
@@ -72,7 +76,7 @@
     lane = lax.broadcasted_iota(jnp.int32, (128, 128), 1)
     first = lane <= rho
 
-    def chunk(j, _):
+    def build(j, into):
         for ch in range(CHANS):
             turned = []
             for b in range(CH + 1):
@@ -83,16 +87,30 @@
                 )
             for b in range(CH):
                 block = jnp.where(first, turned[b], turned[b + 1])
-                hank[ch * 128 : (ch + 1) * 128, b * 128 : (b + 1) * 128] = block.astype(BF16)
-        out = jnp.dot(amat[...], hank[...], preferred_element_type=F32)
+                into[ch * 128 : (ch + 1) * 128, b * 128 : (b + 1) * 128] = block.astype(BF16)
+
+    def multiply(j, held):
+        out = jnp.dot(amat[...], held[...], preferred_element_type=F32)
         for g in range(NQ * NT // 8):
             for b in range(CH):
                 part[pl.ds(g * 8 * NBLK + j * CH + b, 8, stride=NBLK), :] = out[
                     g * 8 : (g + 1) * 8, b * 128 : (b + 1) * 128
                 ]
+
+    def chunks(i, _):
+        for k in range(10):
+            greet(1 + i * 10 + k)
+        multiply(2 * i, hank)
+        build(2 * i + 1, hank2)
+        multiply(2 * i + 1, hank2)
+        build(2 * i + 2, hank)
         return 0
 
-    lax.fori_loop(0, NBLK // CH, chunk, 0)
+    for i in range(61, 64):
+        greet(i)
+    build(0, hank)
+    lax.fori_loop(0, NBLK // CH // 2, chunks, 0)
+    multiply(NBLK // CH - 1, hank)
 
     lane24 = lax.broadcasted_iota(jnp.int32, (ROWS, 128), 1)
 
@@ -264,22 +282,39 @@
     pltpu.make_async_copy(outr.at[pl.ds(0, 63)], got.at[pl.ds(0, 63)], sem_os).wait()
 
 
+def put_out(a, b, c, a_out, b_out, c_out, sems):
+    copies = [
+        pltpu.make_async_copy(one, two, sems.at[i])
+        for i, (one, two) in enumerate(((a, a_out), (b, b_out), (c, c_out)))
+    ]
+    for copy in copies:
+        copy.start()
+    for copy in copies:
+        copy.wait()
+
+
 def on_device(waveform, templates, lags, present):
     vmem = pl.BlockSpec(memory_space=pltpu.VMEM)
-    smem = pl.BlockSpec(memory_space=pltpu.SMEM)
     dma = pltpu.SemaphoreType.DMA
-    score, mad, peak = pl.pallas_call(
+    hbm = pl.BlockSpec(memory_space=pltpu.HBM)
+    results = pl.pallas_call(
         kernel,
         out_shape=(
             jax.ShapeDtypeStruct((OWN, NT), F32),
             jax.ShapeDtypeStruct((1, NT), F32),
             jax.ShapeDtypeStruct((1, OWN), F32),
         ),
-        in_specs=[vmem, vmem, smem, smem],
+        in_specs=[hbm, hbm, hbm, hbm],
         out_specs=(vmem, vmem, vmem),
         scratch_shapes=[
+            pltpu.VMEM((CHANS, SAMPLES), BF16),
+            pltpu.VMEM((NT, CHANS * LEN), BF16),
+            pltpu.SMEM((1, NT), jnp.int32),
+            pltpu.SMEM((1, NT), jnp.int32),
+            dma((4,)),
             pltpu.VMEM((8, (NBLK + 1) * 128), F32),
             pltpu.VMEM((NQ * NT, CHANS * TAPS), BF16),
+            pltpu.VMEM((CHANS * TAPS, CH * 128), BF16),
             pltpu.VMEM((CHANS * TAPS, CH * 128), BF16),
             pltpu.VMEM((NQ * NT * NBLK, 128), F32),
             pltpu.VMEM((NT, 128), F32),
@@ -298,8 +333,20 @@
             dma(()), dma(()), dma((7,)), dma((7,)),
         ],
         compiler_params=pltpu.CompilerParams(
-            collective_id=0, has_side_effects=True, vmem_limit_bytes=50 * 1024 * 1024),
+            collective_id=0, has_side_effects=True, vmem_limit_bytes=56500000),
     )(waveform[0], templates[:, 0, :], lags.reshape(1, NT), present.reshape(1, NT))
+    score, mad, peak = pl.pallas_call(
+        put_out,
+        out_shape=(
+            jax.ShapeDtypeStruct((OWN, NT), F32),
+            jax.ShapeDtypeStruct((1, NT), F32),
+            jax.ShapeDtypeStruct((1, OWN), F32),
+        ),
+        in_specs=[vmem, vmem, vmem],
+        out_specs=(hbm, hbm, hbm),
+        scratch_shapes=[dma((3,))],
+        compiler_params=pltpu.CompilerParams(vmem_limit_bytes=1024 * 1024),
+    )(*results)
     return score, mad[0], peak[0]
 
 

time: 49.5 us -> 46.5 us (0.939)
  local copies, waits for them, and re-layouts: 4.02 us -> 0.66 us
  Pallas kernels: 44.6 us -> 45.1 us
    unnamed x11 -> x4, local copies, waits for them, and re-layouts: 4.02 us -> 0.66 us
    pallas_call x0 -> x1, Pallas kernels: none -> 0.64 us  [on_device(): pl.pallas_call(put_out, out_shape=(jax.ShapeDtypeStruct((OWN, NT), F32),...]
where the time goes in v2:
time: 46.5 us; the launch traced here: 46.4 us
  Pallas kernels  45.1 us (97%)
  local copies, waits for them, and re-layouts  0.66 us (1%)
  between operations  0.66 us (1%)
    pallas_call x1, Pallas kernels, on_device(): pl.pallas_call(kernel, out_shape=(jax.ShapeDtypeStruct((OWN, NT), F32), j...  44.4 us

profile of v2, /device:TPU:1, one launch (start us, length us, event | category | flops | bytes accessed | tf_op | source)
XLA Modules:
  0.0 46.4 jit_solution(10956368294761679471)
XLA Ops:
  0.6 0.0 copy-start
  0.6 0.0 copy-start.1
  0.7 0.6 %copy-done = s32[64,1]{0,1:T(1,128)S(1)} copy-done((s32[64,1]{0,1:T(1,128)S(1)}, s32[64,1]{0,1:T(1,128)}, u32[]{:S(2)}) %copy-start) | copy-done | bytes 280
  1.3 0.0 copy-done.1
  1.3 44.4 %shard_map.67 = (f32[48,64]{1,0:T(8,128)S(1)}, f32[1,64]{1,0:T(1,128)S(1)}, f32[1,48]{1,0:T(1,128)S(1)}) custom-call(bf16[3,6583]{1,0:T(4,128)(2,1)} %bitcast.9, bf16[64,1536]{1,0:T(8,128)(2,1)} %bitcast.8, s32[1,64]{1,0:T(1,128)S(1)} %bitcast.6, s32[1,64]{1,0:T(1,128)S(1)} %bitcast.7), custom_call_target="tpu_custom_call" | custom-call | tf_op jit(solution)/shard_map/pallas_call | solution.py:300
  45.7 0.6 %shard_map.68 = (f32[48,64]{1,0:T(8,128)}, f32[1,64]{1,0:T(1,128)}, f32[1,48]{1,0:T(1,128)}) custom-call(f32[48,64]{1,0:T(8,128)S(1)} %get-tuple-element.9.a, f32[1,64]{1,0:T(1,128)S(1)} %get-tuple-element.10.b, f32[1,48]{1,0:T(1,128)S(1)} %get-tuple-element.11.c), custom_call_target="tpu_custom_call" | custom-call | tf_op jit(solution)/shard_map/pallas_call | solution.py:338
Async XLA Ops:
  0.6 0.7 %copy-start = (s32[64,1]{0,1:T(1,128)S(1)}, s32[64,1]{0,1:T(1,128)}, u32[]{:S(2)}) copy-start(s32[64,1]{0,1:T(1,128)} %param.6) | copy-start | bytes 772
  0.6 0.7 %copy-start.1 = (s32[64,1]{0,1:T(1,128)S(1)}, s32[64,1]{0,1:T(1,128)}, u32[]{:S(2)}) copy-start(s32[64,1]{0,1:T(1,128)} %param.7) | copy-start | bytes 772

commit v3 on v2

--- a/solution.py
+++ b/solution.py
@@ -22,6 +22,7 @@
 F32 = jnp.float32
 BF16 = jnp.bfloat16
 MESH = pl.DeviceIdType.MESH
+AWAY = (4, 3, 5, 2, 6, 1, 7, 0)
 
 
 def kernel(
@@ -49,9 +50,10 @@
     barrier = pltpu.get_barrier_semaphore()
     for i in range(1, 8):
         pl.semaphore_signal(barrier, inc=1, device_id=(s, (tp + i) % 8), device_id_type=MESH)
-
-    def greet(i):
-        pl.semaphore_signal(barrier, inc=1, device_id=((s + i) % 64, tp), device_id_type=MESH)
+        pl.semaphore_signal(barrier, inc=1, device_id=dev(x, (z + i) % 8, c), device_id_type=MESH)
+    for i in range(1, 4):
+        pl.semaphore_signal(barrier, inc=1, device_id=dev((x + i) % 4, z, c), device_id_type=MESH)
+    pl.semaphore_signal(barrier, inc=1, device_id=dev(x, z, 1 - c), device_id_type=MESH)
 
     wrow[...] = jnp.zeros(wrow.shape, F32)
     for copy in inputs:
@@ -98,16 +100,12 @@
                 ]
 
     def chunks(i, _):
-        for k in range(10):
-            greet(1 + i * 10 + k)
         multiply(2 * i, hank)
         build(2 * i + 1, hank2)
         multiply(2 * i + 1, hank2)
         build(2 * i + 2, hank)
         return 0
 
-    for i in range(61, 64):
-        greet(i)
     build(0, hank)
     lax.fori_loop(0, NBLK // CH // 2, chunks, 0)
     multiply(NBLK // CH - 1, hank)
@@ -128,65 +126,55 @@
         left, right = pltpu.roll(left, by, 1), pltpu.roll(right, by, 1)
         return jnp.where(lane24 < 128 - r, left, right) * (scl[pl.ds(t, 1), :] * here)
 
-    def copy_c(d):
-        return pltpu.make_async_remote_copy(
-            src_ref=sendc.at[d], dst_ref=recvc.at[d], send_sem=sem_cs.at[d], recv_sem=sem_cr.at[d],
+    def place(k):
+        return (z + 4 + k // 2 - (k % 2) * k + 8) % 8
+
+    def copy_c(k):
+        return pltpu.make_async_remote_copy(
+            src_ref=sendc.at[k], dst_ref=recvc.at[k], send_sem=sem_cs.at[k], recv_sem=sem_cr.at[k],
             device_id=dev(x, z, 1 - c), device_id_type=MESH)
 
-    def copy_x(d):
-        return pltpu.make_async_remote_copy(
-            src_ref=sendx.at[d - 1], dst_ref=recvx.at[d - 1], send_sem=sem_xs.at[d - 1],
-            recv_sem=sem_xr.at[d - 1], device_id=dev((x + d) % 4, z, c), device_id_type=MESH)
-
-    def copy_z(d):
-        return pltpu.make_async_remote_copy(
-            src_ref=sendz.at[d - 1], dst_ref=recvz.at[d - 1], send_sem=sem_zs.at[d - 1],
-            recv_sem=sem_zr.at[d - 1], device_id=dev(x, (z + d) % 8, c), device_id_type=MESH)
-
-    def fold(d):
-        copy_c(d).wait_recv()
-        if d > 0:
-            sendx[d - 1] = own[d] + recvc[d]
-            copy_x(d).start()
-
-    previous = None
-    for d in (2, 1, 3, 0):
-        base = ((x + d) % 4) * 16
-
-        def theirs(i, _):
-            for k in range(4):
-                zz = i * 4 + k
-                sendc[d, zz] = shifted(base + zz * 2 + 1 - c)
-            return 0
-
-        def ours(i, _):
-            for k in range(4):
-                zz = i * 4 + k
-                own[d, zz] = shifted(base + zz * 2 + c)
-            return 0
-
-        lax.fori_loop(0, 2, theirs, 0)
-        if previous is None:
-            pl.semaphore_wait(barrier, 63 + 7)
-        copy_c(d).start()
-        lax.fori_loop(0, 2, ours, 0)
-        if previous is not None:
-            fold(previous)
-        previous = d
-    fold(0)
-    for d in (1, 3, 2):
-        copy_x(d).wait_recv()
-
-    def reduced(zz):
-        return (own[0, zz] + recvc[0, zz]) + (recvx[0, zz] + recvx[1, zz] + recvx[2, zz])
-
-    for d in (4, 3, 5, 2, 6, 1, 7):
-        sendz[d - 1] = reduced((z + d) % 8)
-        copy_z(d).start()
-    row = reduced(z)
-    for d in (1, 7, 2, 6, 3, 5, 4):
-        copy_z(d).wait_recv()
-        row = row + recvz[d - 1]
+    def copy_x(k, d):
+        return pltpu.make_async_remote_copy(
+            src_ref=sendx.at[k, d - 1], dst_ref=recvx.at[k, d - 1],
+            send_sem=sem_xs.at[k, d - 1], recv_sem=sem_xr.at[k, d - 1],
+            device_id=dev((x + d) % 4, z, c), device_id_type=MESH)
+
+    def copy_z(k):
+        return pltpu.make_async_remote_copy(
+            src_ref=sendz.at[k], dst_ref=recvz.at[k], send_sem=sem_zs.at[k], recv_sem=sem_zr.at[k],
+            device_id=dev(x, (z + AWAY[k]) % 8, c), device_id_type=MESH)
+
+    def theirs(k, _):
+        for d in range(4):
+            sendc[k, d] = shifted(((x + d) % 4) * 16 + place(k) * 2 + 1 - c)
+        copy_c(k).start()
+        return 0
+
+    def ours(k, _):
+        for d in range(4):
+            own[k, d] = shifted(((x + d) % 4) * 16 + place(k) * 2 + c)
+        return 0
+
+    pl.semaphore_wait(barrier, 1 + 3 + 7 + 7)
+    lax.fori_loop(0, 8, theirs, 0)
+    lax.fori_loop(0, 8, ours, 0)
+    for k in range(8):
+        copy_c(k).wait_recv()
+        for d in (2, 1, 3):
+            sendx[k, d - 1] = own[k, d] + recvc[k, d]
+            copy_x(k, d).start()
+    row = None
+    for k in range(8):
+        for d in (1, 3, 2):
+            copy_x(k, d).wait_recv()
+        row = (own[k, 0] + recvc[k, 0]) + (recvx[k, 0] + recvx[k, 1] + recvx[k, 2])
+        if k < 7:
+            sendz[k] = row
+            copy_z(k).start()
+    for k in range(7):
+        copy_z(k).wait_recv()
+        row = row + recvz[k]
 
     pos = jnp.clip(jnp.abs(row) * (BINS / 512.0) - 0.5, 0.0, BINS - 1.0)
     low = jnp.minimum(jnp.floor(pos), BINS - 2.0)
@@ -238,18 +226,26 @@
         for g in range(8):
             outr[8 * g + j] = piece[g : g + 1, :]
 
-    def copy_o(i):
-        to = (s + i) % 64
+    def copy_o(xx, zz, cc):
+        to = xx * 16 + zz * 2 + cc
         return pltpu.make_async_remote_copy(
             src_ref=outr.at[to], dst_ref=got.at[s], send_sem=sem_os, recv_sem=sem_or,
             device_id=(to, tp), device_id_type=MESH)
 
-    def send(i, _):
-        copy_o((i + 32) % 64).start()
+    others = [(x + d) % 4 for d in range(4)]
+
+    def send(k, _):
+        zz = place(k)
+        for d in (2, 1, 3, 0):
+            copy_o(others[d], zz, c).start()
+            copy_o(others[d], zz, 1 - c).start()
         return 0
 
-    lax.fori_loop(0, 32, send, 0)
-    lax.fori_loop(33, 64, send, 0)
+    lax.fori_loop(0, 7, send, 0)
+    for d in (2, 1, 3):
+        copy_o(others[d], z, c).start()
+        copy_o(others[d], z, 1 - c).start()
+    copy_o(x, z, 1 - c).start()
     got[s] = outr[s]
     pltpu.make_async_copy(outr.at[pl.ds(0, 63)], got.at[pl.ds(0, 63)], sem_or).wait()
 
@@ -272,13 +268,13 @@
         best = jnp.maximum(best, pkgot[d])
     peak_ref[...] = best[:, 0:OWN]
 
-    for d in range(4):
-        copy_c(d).wait_send()
-    for d in range(1, 4):
-        copy_x(d).wait_send()
-    for d in range(1, 8):
-        copy_z(d).wait_send()
-        copy_p(d).wait_send()
+    for k in range(8):
+        copy_c(k).wait_send()
+        for d in range(1, 4):
+            copy_x(k, d).wait_send()
+    for k in range(7):
+        copy_z(k).wait_send()
+        copy_p(k + 1).wait_send()
     pltpu.make_async_copy(outr.at[pl.ds(0, 63)], got.at[pl.ds(0, 63)], sem_os).wait()
 
 
@@ -318,18 +314,18 @@
             pltpu.VMEM((CHANS * TAPS, CH * 128), BF16),
             pltpu.VMEM((NQ * NT * NBLK, 128), F32),
             pltpu.VMEM((NT, 128), F32),
-            pltpu.VMEM((4, 8, ROWS, 128), F32),
-            pltpu.VMEM((4, 8, ROWS, 128), F32),
-            pltpu.VMEM((4, 8, ROWS, 128), F32),
-            pltpu.VMEM((3, 8, ROWS, 128), F32),
-            pltpu.VMEM((3, 8, ROWS, 128), F32),
+            pltpu.VMEM((8, 4, ROWS, 128), F32),
+            pltpu.VMEM((8, 4, ROWS, 128), F32),
+            pltpu.VMEM((8, 4, ROWS, 128), F32),
+            pltpu.VMEM((8, 3, ROWS, 128), F32),
+            pltpu.VMEM((8, 3, ROWS, 128), F32),
             pltpu.VMEM((7, ROWS, 128), F32),
             pltpu.VMEM((7, ROWS, 128), F32),
             pltpu.VMEM((64, 1, 128), F32),
             pltpu.VMEM((64, 1, 128), F32),
             pltpu.VMEM((ROWS, 128), F32),
             pltpu.VMEM((8, 1, 128), F32),
-            dma((4,)), dma((4,)), dma((3,)), dma((3,)), dma((7,)), dma((7,)),
+            dma((8,)), dma((8,)), dma((8, 3)), dma((8, 3)), dma((7,)), dma((7,)),
             dma(()), dma(()), dma((7,)), dma((7,)),
         ],
         compiler_params=pltpu.CompilerParams(

time: 46.5 us -> 41.1 us (0.88)
  Pallas kernels: 45.1 us -> 39.6 us
    pallas_call x1, Pallas kernels: 44.4 us -> 39 us  [on_device(): pl.pallas_call(kernel, out_shape=(jax.ShapeDtypeStruct((OWN, NT), F32), j...]
where the time goes in v3:
time: 41.1 us; the launch traced here: 40.9 us
  Pallas kernels  39.6 us (96%)
  local copies, waits for them, and re-layouts  0.66 us (2%)
  between operations  0.66 us (2%)
    pallas_call x1, Pallas kernels, on_device(): pl.pallas_call(kernel, out_shape=(jax.ShapeDtypeStruct((OWN, NT), F32), j...  39 us

profile of v3, /device:TPU:1, one launch (start us, length us, event | category | flops | bytes accessed | tf_op | source)
XLA Modules:
  0.0 40.9 jit_solution(17538462106323871811)
XLA Ops:
  0.6 0.0 copy-start
  0.6 0.0 copy-start.1
  0.7 0.6 %copy-done = s32[64,1]{0,1:T(1,128)S(1)} copy-done((s32[64,1]{0,1:T(1,128)S(1)}, s32[64,1]{0,1:T(1,128)}, u32[]{:S(2)}) %copy-start) | copy-done | bytes 280
  1.3 0.0 copy-done.1
  1.3 39.0 %shard_map.67 = (f32[48,64]{1,0:T(8,128)S(1)}, f32[1,64]{1,0:T(1,128)S(1)}, f32[1,48]{1,0:T(1,128)S(1)}) custom-call(bf16[3,6583]{1,0:T(4,128)(2,1)} %bitcast.9, bf16[64,1536]{1,0:T(8,128)(2,1)} %bitcast.8, s32[1,64]{1,0:T(1,128)S(1)} %bitcast.6, s32[1,64]{1,0:T(1,128)S(1)} %bitcast.7), custom_call_target="tpu_custom_call" | custom-call | tf_op jit(solution)/shard_map/pallas_call | solution.py:296
  40.3 0.6 %shard_map.68 = (f32[48,64]{1,0:T(8,128)}, f32[1,64]{1,0:T(1,128)}, f32[1,48]{1,0:T(1,128)}) custom-call(f32[48,64]{1,0:T(8,128)S(1)} %get-tuple-element.9.a, f32[1,64]{1,0:T(1,128)S(1)} %get-tuple-element.10.b, f32[1,48]{1,0:T(1,128)S(1)} %get-tuple-element.11.c), custom_call_target="tpu_custom_call" | custom-call | tf_op jit(solution)/shard_map/pallas_call | solution.py:334
Async XLA Ops:
  0.6 0.7 %copy-start = (s32[64,1]{0,1:T(1,128)S(1)}, s32[64,1]{0,1:T(1,128)}, u32[]{:S(2)}) copy-start(s32[64,1]{0,1:T(1,128)} %param.6) | copy-start | bytes 772
  0.6 0.7 %copy-start.1 = (s32[64,1]{0,1:T(1,128)S(1)}, s32[64,1]{0,1:T(1,128)}, u32[]{:S(2)}) copy-start(s32[64,1]{0,1:T(1,128)} %param.7) | copy-start | bytes 772

commit v4 on v3

--- a/solution.py
+++ b/solution.py
@@ -55,79 +55,96 @@
         pl.semaphore_signal(barrier, inc=1, device_id=dev((x + i) % 4, z, c), device_id_type=MESH)
     pl.semaphore_signal(barrier, inc=1, device_id=dev(x, z, 1 - c), device_id_type=MESH)
 
+    def place(k):
+        return (z + 4 + k // 2 - (k % 2) * k + 8) % 8
+
+    spot = lax.broadcasted_iota(jnp.int32, (NT, NT), 0)
+    column = lax.broadcasted_iota(jnp.int32, (NT, NT), 1)
+    step, turn, mine = spot >> 3, (spot >> 1) & 3, spot & 1
+    source = (((x + turn) & 3) * 16 + ((z + 4 + (step >> 1) - (step & 1) * step + 8) & 7) * 2
+              + (c + 1 - mine) % 2)
+    order = jnp.where(source == column, 1.0, 0.0).astype(BF16)
+    flip_i = lax.broadcasted_iota(jnp.int32, (128, 128), 0)
+    flip_j = lax.broadcasted_iota(jnp.int32, (128, 128), 1)
+    flip = jnp.where(flip_i + flip_j == 127, 1.0, 0.0).astype(BF16)
+
     wrow[...] = jnp.zeros(wrow.shape, F32)
     for copy in inputs:
         copy.wait()
     wrow[0:CHANS, 0:SAMPLES] = wave_ref[...].astype(F32)
 
     total = jnp.zeros((NT, 128), F32)
-    flip_i = lax.broadcasted_iota(jnp.int32, (128, 128), 0)
-    flip_j = lax.broadcasted_iota(jnp.int32, (128, 128), 1)
-    flip = jnp.where(flip_i + flip_j == 127, 1.0, 0.0).astype(BF16)
     for ch in range(CHANS):
         for q in range(NQ):
-            piece = temp_ref[:, (ch * NQ + q) * 128 : (ch * NQ + q + 1) * 128]
-            wide = piece.astype(F32)
+            wide = jnp.dot(
+                order, temp_ref[:, (ch * NQ + q) * 128 : (ch * NQ + q + 1) * 128],
+                preferred_element_type=F32)
             total = total + wide * wide
-            turned = jnp.dot(piece, flip, preferred_element_type=F32).astype(BF16)
-            amat[q * NT : (q + 1) * NT, ch * 128 : (ch + 1) * 128] = turned
+            turned = jnp.dot(wide.astype(BF16), flip, preferred_element_type=F32).astype(BF16)
+            for half in range(2):
+                amat[half, q * 32 : (q + 1) * 32, ch * 128 : (ch + 1) * 128] = turned[
+                    half * 32 : (half + 1) * 32, :
+                ]
     norm = jnp.sqrt(jnp.sum(total, axis=1, keepdims=True) + 1e-6)
     scl[...] = jnp.broadcast_to(1.0 / norm, (NT, 128))
 
-    rho = lax.broadcasted_iota(jnp.int32, (128, 128), 0)
-    lane = lax.broadcasted_iota(jnp.int32, (128, 128), 1)
-    first = lane <= rho
-
-    def build(j, into):
+    rho = lax.broadcasted_iota(jnp.int32, (16, 128), 0)
+    lane16 = lax.broadcasted_iota(jnp.int32, (16, 128), 1)
+
+    def build(j, into, slot):
         for ch in range(CHANS):
-            turned = []
-            for b in range(CH + 1):
-                at = pl.multiple_of((j * CH + b) * 128, 128)
-                row = wrow[ch : ch + 1, pl.ds(at, 128)]
-                turned.append(
-                    pltpu.roll(jnp.broadcast_to(row, (128, 128)), 1, 1, stride=1, stride_axis=0)
-                )
+            for g in range(TAPS // 16):
+                first = lane16 <= rho + 16 * g
+                before = None
+                for b in range(CH + 1):
+                    at = pl.multiple_of((j * CH + b) * 128, 128)
+                    row = jnp.broadcast_to(wrow[ch : ch + 1, pl.ds(at, 128)], (16, 128))
+                    after = pltpu.roll(row, 1 + 16 * g, 1, stride=1, stride_axis=0)
+                    if b:
+                        into[
+                            slot,
+                            ch * TAPS + g * 16 : ch * TAPS + (g + 1) * 16,
+                            (b - 1) * 128 : b * 128,
+                        ] = jnp.where(first, before, after).astype(BF16)
+                    before = after
+
+    def multiply(half, j, held, slot):
+        out = jnp.dot(amat[half], held[slot], preferred_element_type=F32)
+        for g in range(NQ * 4):
             for b in range(CH):
-                block = jnp.where(first, turned[b], turned[b + 1])
-                into[ch * 128 : (ch + 1) * 128, b * 128 : (b + 1) * 128] = block.astype(BF16)
-
-    def multiply(j, held):
-        out = jnp.dot(amat[...], held[...], preferred_element_type=F32)
-        for g in range(NQ * NT // 8):
-            for b in range(CH):
-                part[pl.ds(g * 8 * NBLK + j * CH + b, 8, stride=NBLK), :] = out[
+                part[pl.ds((half * NQ * 4 + g) * 8 * NBLK + j * CH + b, 8, stride=NBLK), :] = out[
                     g * 8 : (g + 1) * 8, b * 128 : (b + 1) * 128
                 ]
 
-    def chunks(i, _):
-        multiply(2 * i, hank)
-        build(2 * i + 1, hank2)
-        multiply(2 * i + 1, hank2)
-        build(2 * i + 2, hank)
-        return 0
-
-    build(0, hank)
-    lax.fori_loop(0, NBLK // CH // 2, chunks, 0)
-    multiply(NBLK // CH - 1, hank)
+    def first_half(i, _):
+        multiply(0, 2 * i, hank, i)
+        build(2 * i + 1, hank2, i)
+        multiply(0, 2 * i + 1, hank2, i)
+        build(2 * i + 2, hank, i + 1)
+        return 0
+
+    def second_half(i, _):
+        multiply(1, 2 * i, hank, i)
+        multiply(1, 2 * i + 1, hank2, i)
+        return 0
 
     lane24 = lax.broadcasted_iota(jnp.int32, (ROWS, 128), 1)
 
-    def shifted(t):
+    def shifted(k, d, mine):
+        t = ((x + d) % 4) * 16 + place(k) * 2 + (c if mine else 1 - c)
         lag = lag_ref[0, t]
         here = pres_ref[0, t].astype(F32)
         a, r = lag // 128, lag % 128
         left = right = None
         for q in range(NQ):
-            at = (q * NT + t) * NBLK + q + a
+            at = ((k // 4) * NQ * 32 + q * 32 + (k % 4) * 8 + 2 * d + mine) * NBLK + q + a
             one, two = part[pl.ds(at, ROWS), :], part[pl.ds(at + 1, ROWS), :]
             left = one if left is None else left + one
             right = two if right is None else right + two
         by = (128 - r) % 128
         left, right = pltpu.roll(left, by, 1), pltpu.roll(right, by, 1)
-        return jnp.where(lane24 < 128 - r, left, right) * (scl[pl.ds(t, 1), :] * here)
-
-    def place(k):
-        return (z + 4 + k // 2 - (k % 2) * k + 8) % 8
+        scale = scl[pl.ds(k * 8 + 2 * d + mine, 1), :] * here
+        return jnp.where(lane24 < 128 - r, left, right) * scale
 
     def copy_c(k):
         return pltpu.make_async_remote_copy(
@@ -147,23 +164,36 @@
 
     def theirs(k, _):
         for d in range(4):
-            sendc[k, d] = shifted(((x + d) % 4) * 16 + place(k) * 2 + 1 - c)
+            sendc[k, d] = shifted(k, d, 0)
         copy_c(k).start()
         return 0
 
     def ours(k, _):
         for d in range(4):
-            own[k, d] = shifted(((x + d) % 4) * 16 + place(k) * 2 + c)
-        return 0
-
-    pl.semaphore_wait(barrier, 1 + 3 + 7 + 7)
-    lax.fori_loop(0, 8, theirs, 0)
-    lax.fori_loop(0, 8, ours, 0)
-    for k in range(8):
+            own[k, d] = shifted(k, d, 1)
+        return 0
+
+    def fold(k):
         copy_c(k).wait_recv()
         for d in (2, 1, 3):
             sendx[k, d - 1] = own[k, d] + recvc[k, d]
             copy_x(k, d).start()
+
+    build(0, hank, 0)
+    lax.fori_loop(0, NBLK // CH // 2, first_half, 0)
+    multiply(0, NBLK // CH - 1, hank, NBLK // CH // 2)
+    pl.semaphore_wait(barrier, 1 + 3 + 7 + 7)
+    lax.fori_loop(0, 4, theirs, 0)
+    lax.fori_loop(0, 4, ours, 0)
+    lax.fori_loop(0, 4, second_half, 0)
+    for k in range(4):
+        fold(k)
+    lax.fori_loop(4, NBLK // CH // 2, second_half, 0)
+    multiply(1, NBLK // CH - 1, hank, NBLK // CH // 2)
+    lax.fori_loop(4, 8, theirs, 0)
+    lax.fori_loop(4, 8, ours, 0)
+    for k in range(4, 8):
+        fold(k)
     row = None
     for k in range(8):
         for d in (1, 3, 2):
@@ -309,9 +339,9 @@
             pltpu.SMEM((1, NT), jnp.int32),
             dma((4,)),
             pltpu.VMEM((8, (NBLK + 1) * 128), F32),
-            pltpu.VMEM((NQ * NT, CHANS * TAPS), BF16),
-            pltpu.VMEM((CHANS * TAPS, CH * 128), BF16),
-            pltpu.VMEM((CHANS * TAPS, CH * 128), BF16),
+            pltpu.VMEM((2, NQ * 32, CHANS * TAPS), BF16),
+            pltpu.VMEM((NBLK // CH // 2 + 1, CHANS * TAPS, CH * 128), BF16),
+            pltpu.VMEM((NBLK // CH // 2, CHANS * TAPS, CH * 128), BF16),
             pltpu.VMEM((NQ * NT * NBLK, 128), F32),
             pltpu.VMEM((NT, 128), F32),
             pltpu.VMEM((8, 4, ROWS, 128), F32),

time: 41.1 us -> 41.6 us (1.012)
  Pallas kernels: 39.6 us -> 40.2 us
    pallas_call x1, Pallas kernels: 39 us -> 39.5 us  [on_device(): pl.pallas_call(kernel, out_shape=(jax.ShapeDtypeStruct((OWN, NT), F32), j...]
where the time goes in v4:
time: 41.6 us; the launch traced here: 41.5 us
  Pallas kernels  40.2 us (97%)
  local copies, waits for them, and re-layouts  0.66 us (2%)
  between operations  0.66 us (2%)
    pallas_call x1, Pallas kernels, on_device(): pl.pallas_call(kernel, out_shape=(jax.ShapeDtypeStruct((OWN, NT), F32), j...  39.5 us

profile of v4, /device:TPU:1, one launch (start us, length us, event | category | flops | bytes accessed | tf_op | source)
XLA Modules:
  0.0 41.5 jit_solution(5631914220053762475)
XLA Ops:
  0.6 0.0 copy-start
  0.6 0.0 copy-start.1
  0.7 0.6 %copy-done = s32[64,1]{0,1:T(1,128)S(1)} copy-done((s32[64,1]{0,1:T(1,128)S(1)}, s32[64,1]{0,1:T(1,128)}, u32[]{:S(2)}) %copy-start) | copy-done | bytes 280
  1.3 0.0 copy-done.1
  1.3 39.5 %shard_map.67 = (f32[48,64]{1,0:T(8,128)S(1)}, f32[1,64]{1,0:T(1,128)S(1)}, f32[1,48]{1,0:T(1,128)S(1)}) custom-call(bf16[3,6583]{1,0:T(4,128)(2,1)} %bitcast.9, bf16[64,1536]{1,0:T(8,128)(2,1)} %bitcast.8, s32[1,64]{1,0:T(1,128)S(1)} %bitcast.6, s32[1,64]{1,0:T(1,128)S(1)} %bitcast.7), custom_call_target="tpu_custom_call" | custom-call | tf_op jit(solution)/shard_map/pallas_call | solution.py:326
  40.9 0.6 %shard_map.68 = (f32[48,64]{1,0:T(8,128)}, f32[1,64]{1,0:T(1,128)}, f32[1,48]{1,0:T(1,128)}) custom-call(f32[48,64]{1,0:T(8,128)S(1)} %get-tuple-element.9.a, f32[1,64]{1,0:T(1,128)S(1)} %get-tuple-element.10.b, f32[1,48]{1,0:T(1,128)S(1)} %get-tuple-element.11.c), custom_call_target="tpu_custom_call" | custom-call | tf_op jit(solution)/shard_map/pallas_call | solution.py:364
Async XLA Ops:
  0.6 0.7 %copy-start = (s32[64,1]{0,1:T(1,128)S(1)}, s32[64,1]{0,1:T(1,128)}, u32[]{:S(2)}) copy-start(s32[64,1]{0,1:T(1,128)} %param.6) | copy-start | bytes 772
  0.6 0.7 %copy-start.1 = (s32[64,1]{0,1:T(1,128)S(1)}, s32[64,1]{0,1:T(1,128)}, u32[]{:S(2)}) copy-start(s32[64,1]{0,1:T(1,128)} %param.7) | copy-start | bytes 772

commit v5 on v3

--- a/solution.py
+++ b/solution.py
@@ -74,22 +74,24 @@
     norm = jnp.sqrt(jnp.sum(total, axis=1, keepdims=True) + 1e-6)
     scl[...] = jnp.broadcast_to(1.0 / norm, (NT, 128))
 
-    rho = lax.broadcasted_iota(jnp.int32, (128, 128), 0)
-    lane = lax.broadcasted_iota(jnp.int32, (128, 128), 1)
-    first = lane <= rho
+    rho = lax.broadcasted_iota(jnp.int32, (16, 128), 0)
+    lane16 = lax.broadcasted_iota(jnp.int32, (16, 128), 1)
 
     def build(j, into):
         for ch in range(CHANS):
-            turned = []
-            for b in range(CH + 1):
-                at = pl.multiple_of((j * CH + b) * 128, 128)
-                row = wrow[ch : ch + 1, pl.ds(at, 128)]
-                turned.append(
-                    pltpu.roll(jnp.broadcast_to(row, (128, 128)), 1, 1, stride=1, stride_axis=0)
-                )
-            for b in range(CH):
-                block = jnp.where(first, turned[b], turned[b + 1])
-                into[ch * 128 : (ch + 1) * 128, b * 128 : (b + 1) * 128] = block.astype(BF16)
+            for g in range(TAPS // 16):
+                first = lane16 <= rho + 16 * g
+                before = None
+                for b in range(CH + 1):
+                    at = pl.multiple_of((j * CH + b) * 128, 128)
+                    row = jnp.broadcast_to(wrow[ch : ch + 1, pl.ds(at, 128)], (16, 128))
+                    after = pltpu.roll(row, 1 + 16 * g, 1, stride=1, stride_axis=0)
+                    if b:
+                        into[
+                            ch * TAPS + g * 16 : ch * TAPS + (g + 1) * 16,
+                            (b - 1) * 128 : b * 128,
+                        ] = jnp.where(first, before, after).astype(BF16)
+                    before = after
 
     def multiply(j, held):
         out = jnp.dot(amat[...], held[...], preferred_element_type=F32)
@@ -145,25 +147,30 @@
             src_ref=sendz.at[k], dst_ref=recvz.at[k], send_sem=sem_zs.at[k], recv_sem=sem_zr.at[k],
             device_id=dev(x, (z + AWAY[k]) % 8, c), device_id_type=MESH)
 
-    def theirs(k, _):
+    def both(k, _):
         for d in range(4):
             sendc[k, d] = shifted(((x + d) % 4) * 16 + place(k) * 2 + 1 - c)
         copy_c(k).start()
-        return 0
-
-    def ours(k, _):
         for d in range(4):
             own[k, d] = shifted(((x + d) % 4) * 16 + place(k) * 2 + c)
         return 0
 
-    pl.semaphore_wait(barrier, 1 + 3 + 7 + 7)
-    lax.fori_loop(0, 8, theirs, 0)
-    lax.fori_loop(0, 8, ours, 0)
-    for k in range(8):
+    def fold(k, _):
         copy_c(k).wait_recv()
         for d in (2, 1, 3):
             sendx[k, d - 1] = own[k, d] + recvc[k, d]
             copy_x(k, d).start()
+        return 0
+
+    def both_fold(k, _):
+        both(k, 0)
+        fold(k - 5, 0)
+        return 0
+
+    pl.semaphore_wait(barrier, 1 + 3 + 7 + 7)
+    lax.fori_loop(0, 5, both, 0)
+    lax.fori_loop(5, 8, both_fold, 0)
+    lax.fori_loop(3, 8, fold, 0)
     row = None
     for k in range(8):
         for d in (1, 3, 2):

time: 41.1 us -> 40.6 us (0.988)
  Pallas kernels: 39.6 us -> 39.1 us
    pallas_call x1, Pallas kernels: 39 us -> 38.5 us  [on_device(): pl.pallas_call(kernel, out_shape=(jax.ShapeDtypeStruct((OWN, NT), F32), j...]
where the time goes in v5:
time: 40.6 us; the launch traced here: 40.5 us
  Pallas kernels  39.1 us (96%)
  local copies, waits for them, and re-layouts  0.66 us (2%)
  between operations  0.66 us (2%)
    pallas_call x1, Pallas kernels, on_device(): pl.pallas_call(kernel, out_shape=(jax.ShapeDtypeStruct((OWN, NT), F32), j...  38.5 us

profile of v5, /device:TPU:1, one launch (start us, length us, event | category | flops | bytes accessed | tf_op | source)
XLA Modules:
  0.0 40.5 jit_solution(2049792452995172215)
XLA Ops:
  0.6 0.0 copy-start
  0.6 0.0 copy-start.1
  0.7 0.6 %copy-done = s32[64,1]{0,1:T(1,128)S(1)} copy-done((s32[64,1]{0,1:T(1,128)S(1)}, s32[64,1]{0,1:T(1,128)}, u32[]{:S(2)}) %copy-start) | copy-done | bytes 280
  1.3 0.0 copy-done.1
  1.3 38.5 %shard_map.67 = (f32[48,64]{1,0:T(8,128)S(1)}, f32[1,64]{1,0:T(1,128)S(1)}, f32[1,48]{1,0:T(1,128)S(1)}) custom-call(bf16[3,6583]{1,0:T(4,128)(2,1)} %bitcast.9, bf16[64,1536]{1,0:T(8,128)(2,1)} %bitcast.8, s32[1,64]{1,0:T(1,128)S(1)} %bitcast.6, s32[1,64]{1,0:T(1,128)S(1)} %bitcast.7), custom_call_target="tpu_custom_call" | custom-call | tf_op jit(solution)/shard_map/pallas_call | solution.py:303
  39.8 0.6 %shard_map.68 = (f32[48,64]{1,0:T(8,128)}, f32[1,64]{1,0:T(1,128)}, f32[1,48]{1,0:T(1,128)}) custom-call(f32[48,64]{1,0:T(8,128)S(1)} %get-tuple-element.9.a, f32[1,64]{1,0:T(1,128)S(1)} %get-tuple-element.10.b, f32[1,48]{1,0:T(1,128)S(1)} %get-tuple-element.11.c), custom_call_target="tpu_custom_call" | custom-call | tf_op jit(solution)/shard_map/pallas_call | solution.py:341
Async XLA Ops:
  0.6 0.7 %copy-start = (s32[64,1]{0,1:T(1,128)S(1)}, s32[64,1]{0,1:T(1,128)}, u32[]{:S(2)}) copy-start(s32[64,1]{0,1:T(1,128)} %param.6) | copy-start | bytes 772
  0.6 0.7 %copy-start.1 = (s32[64,1]{0,1:T(1,128)S(1)}, s32[64,1]{0,1:T(1,128)}, u32[]{:S(2)}) copy-start(s32[64,1]{0,1:T(1,128)} %param.7) | copy-start | bytes 772

commit v6 on v5

--- a/solution.py
+++ b/solution.py
@@ -14,8 +14,8 @@
 TOUT = 3072
 NT = 64
 TAPS = 128
-NQ = LEN // TAPS
-NBLK = 52
+NQ = 2
+NBLK = 50
 CH = 4
 ROWS = TOUT // 128
 OWN = TOUT // 64
@@ -27,7 +27,7 @@
 
 def kernel(
     wave_hbm, temp_hbm, lag_hbm, pres_hbm, score_ref, mad_ref, peak_ref,
-    wave_ref, temp_ref, lag_ref, pres_ref, sem_in, wrow, amat, hank, hank2, part, scl, sendc, own, recvc, sendx, recvx, sendz, recvz,
+    wave_ref, temp_ref, lag_ref, pres_ref, sem_in, wrow, amat, hank0, hank1, hank2, part, scl, sendc, own, recvc, sendx, recvx, sendz, recvz,
     outr, got, pk, pkgot,
     sem_cs, sem_cr, sem_xs, sem_xr, sem_zs, sem_zr, sem_os, sem_or, sem_ps, sem_pr,
 ):
@@ -65,21 +65,23 @@
     flip_j = lax.broadcasted_iota(jnp.int32, (128, 128), 1)
     flip = jnp.where(flip_i + flip_j == 127, 1.0, 0.0).astype(BF16)
     for ch in range(CHANS):
-        for q in range(NQ):
-            piece = temp_ref[:, (ch * NQ + q) * 128 : (ch * NQ + q + 1) * 128]
+        for k in range(LEN // TAPS):
+            piece = temp_ref[:, ch * LEN + k * TAPS : ch * LEN + (k + 1) * TAPS]
             wide = piece.astype(F32)
             total = total + wide * wide
             turned = jnp.dot(piece, flip, preferred_element_type=F32).astype(BF16)
-            amat[q * NT : (q + 1) * NT, ch * 128 : (ch + 1) * 128] = turned
+            at = (ch * 2 + k % 2) * TAPS
+            amat[(k // 2) * NT : (k // 2 + 1) * NT, at : at + TAPS] = turned
     norm = jnp.sqrt(jnp.sum(total, axis=1, keepdims=True) + 1e-6)
     scl[...] = jnp.broadcast_to(1.0 / norm, (NT, 128))
 
     rho = lax.broadcasted_iota(jnp.int32, (16, 128), 0)
     lane16 = lax.broadcasted_iota(jnp.int32, (16, 128), 1)
 
-    def build(j, into):
+    def build(j, into, ahead=None):
         for ch in range(CHANS):
             for g in range(TAPS // 16):
+                rows = slice(ch * TAPS + g * 16, ch * TAPS + (g + 1) * 16)
                 first = lane16 <= rho + 16 * g
                 before = None
                 for b in range(CH + 1):
@@ -87,30 +89,45 @@
                     row = jnp.broadcast_to(wrow[ch : ch + 1, pl.ds(at, 128)], (16, 128))
                     after = pltpu.roll(row, 1 + 16 * g, 1, stride=1, stride_axis=0)
                     if b:
-                        into[
-                            ch * TAPS + g * 16 : ch * TAPS + (g + 1) * 16,
-                            (b - 1) * 128 : b * 128,
-                        ] = jnp.where(first, before, after).astype(BF16)
+                        block = jnp.where(first, before, after).astype(BF16)
+                        into[rows, (b - 1) * 128 : b * 128] = block
+                        if b == 1 and ahead is not None:
+                            ahead[rows, CH * 128 : (CH + 1) * 128] = block
                     before = after
 
-    def multiply(j, held):
-        out = jnp.dot(amat[...], held[...], preferred_element_type=F32)
-        for g in range(NQ * NT // 8):
-            for b in range(CH):
-                part[pl.ds(g * 8 * NBLK + j * CH + b, 8, stride=NBLK), :] = out[
-                    g * 8 : (g + 1) * 8, b * 128 : (b + 1) * 128
-                ]
+    def multiply(j, held, tiles=CH // 2):
+        for p in range(tiles):
+            halves = []
+            for ch in range(CHANS):
+                for h in range(2):
+                    at = (2 * p + h) * 128
+                    halves.append(held[ch * TAPS : (ch + 1) * TAPS, at : at + 256])
+            out = jnp.dot(
+                amat[...], jnp.concatenate(halves, axis=0), preferred_element_type=F32)
+            for g in range(NQ * NT // 8):
+                for b in range(2):
+                    part[pl.ds(g * 8 * NBLK + j * CH + 2 * p + b, 8, stride=NBLK), :] = out[
+                        g * 8 : (g + 1) * 8, b * 128 : (b + 1) * 128
+                    ]
 
     def chunks(i, _):
-        multiply(2 * i, hank)
-        build(2 * i + 1, hank2)
-        multiply(2 * i + 1, hank2)
-        build(2 * i + 2, hank)
-        return 0
-
-    build(0, hank)
-    lax.fori_loop(0, NBLK // CH // 2, chunks, 0)
-    multiply(NBLK // CH - 1, hank)
+        multiply(3 * i, hank0)
+        build(3 * i + 2, hank2, hank1)
+        multiply(3 * i + 1, hank1)
+        build(3 * i + 3, hank0, hank2)
+        multiply(3 * i + 2, hank2)
+        build(3 * i + 4, hank1, hank0)
+        return 0
+
+    build(0, hank0)
+    build(1, hank1, hank0)
+    lax.fori_loop(0, 3, chunks, 0)
+    multiply(9, hank0)
+    build(11, hank2, hank1)
+    multiply(10, hank1)
+    build(12, hank0, hank2)
+    multiply(11, hank2)
+    multiply(12, hank0, 1)
 
     lane24 = lax.broadcasted_iota(jnp.int32, (ROWS, 128), 1)
 
@@ -120,7 +137,7 @@
         a, r = lag // 128, lag % 128
         left = right = None
         for q in range(NQ):
-            at = (q * NT + t) * NBLK + q + a
+            at = (q * NT + t) * NBLK + 2 * q + a
             one, two = part[pl.ds(at, ROWS), :], part[pl.ds(at + 1, ROWS), :]
             left = one if left is None else left + one
             right = two if right is None else right + two
@@ -198,12 +215,9 @@
             hats[k].append(near)
             hat = hat - near.astype(F32)
     ones = jnp.concatenate(ones, axis=1)
-    counts = None
-    for k in range(3):
-        got_k = lax.dot_general(
-            jnp.concatenate(hats[k], axis=1), ones, (((1,), (1,)), ((), ())),
-            preferred_element_type=F32)
-        counts = got_k if counts is None else counts + got_k
+    stacked = jnp.concatenate([jnp.concatenate(piece, axis=1) for piece in hats], axis=0)
+    counts = lax.dot_general(stacked, ones, (((1,), (1,)), ((), ())), preferred_element_type=F32)
+    counts = counts[0:40, :] + counts[40:80, :] + counts[80:120, :]
     over = jnp.concatenate([jnp.zeros((1, 1), F32), counts[32:33, 0:31]], axis=1)
     row_l = lax.broadcasted_iota(jnp.int32, (32, 32), 0)
     col_h = lax.broadcasted_iota(jnp.int32, (32, 32), 1)
@@ -315,10 +329,11 @@
             pltpu.SMEM((1, NT), jnp.int32),
             pltpu.SMEM((1, NT), jnp.int32),
             dma((4,)),
-            pltpu.VMEM((8, (NBLK + 1) * 128), F32),
-            pltpu.VMEM((NQ * NT, CHANS * TAPS), BF16),
-            pltpu.VMEM((CHANS * TAPS, CH * 128), BF16),
-            pltpu.VMEM((CHANS * TAPS, CH * 128), BF16),
+            pltpu.VMEM((8, 53 * 128), F32),
+            pltpu.VMEM((NQ * NT, 2 * CHANS * TAPS), BF16),
+            pltpu.VMEM((CHANS * TAPS, (CH + 1) * 128), BF16),
+            pltpu.VMEM((CHANS * TAPS, (CH + 1) * 128), BF16),
+            pltpu.VMEM((CHANS * TAPS, (CH + 1) * 128), BF16),
             pltpu.VMEM((NQ * NT * NBLK, 128), F32),
             pltpu.VMEM((NT, 128), F32),
             pltpu.VMEM((8, 4, ROWS, 128), F32),

time: 40.6 us -> 39.9 us (0.983)
  Pallas kernels: 39.1 us -> 38.5 us
    pallas_call x1, Pallas kernels: 38.5 us -> 37.8 us  [on_device(): pl.pallas_call(kernel, out_shape=(jax.ShapeDtypeStruct((OWN, NT), F32), j...]
where the time goes in v6:
time: 39.9 us; the launch traced here: 39.8 us
  Pallas kernels  38.5 us (96%)
  local copies, waits for them, and re-layouts  0.66 us (2%)
  between operations  0.66 us (2%)
    pallas_call x1, Pallas kernels, on_device(): pl.pallas_call(kernel, out_shape=(jax.ShapeDtypeStruct((OWN, NT), F32), j...  37.8 us

profile of v6, /device:TPU:1, one launch (start us, length us, event | category | flops | bytes accessed | tf_op | source)
XLA Modules:
  0.0 39.8 jit_solution(160735239418328262)
XLA Ops:
  0.6 0.0 copy-start
  0.6 0.0 copy-start.1
  0.7 0.6 %copy-done = s32[64,1]{0,1:T(1,128)S(1)} copy-done((s32[64,1]{0,1:T(1,128)S(1)}, s32[64,1]{0,1:T(1,128)}, u32[]{:S(2)}) %copy-start) | copy-done | bytes 280
  1.3 0.0 copy-done.1
  1.3 37.8 %shard_map.67 = (f32[48,64]{1,0:T(8,128)S(1)}, f32[1,64]{1,0:T(1,128)S(1)}, f32[1,48]{1,0:T(1,128)S(1)}) custom-call(bf16[3,6583]{1,0:T(4,128)(2,1)} %bitcast.9, bf16[64,1536]{1,0:T(8,128)(2,1)} %bitcast.8, s32[1,64]{1,0:T(1,128)S(1)} %bitcast.6, s32[1,64]{1,0:T(1,128)S(1)} %bitcast.7), custom_call_target="tpu_custom_call" | custom-call | tf_op jit(solution)/shard_map/pallas_call | solution.py:317
  39.1 0.6 %shard_map.68 = (f32[48,64]{1,0:T(8,128)}, f32[1,64]{1,0:T(1,128)}, f32[1,48]{1,0:T(1,128)}) custom-call(f32[48,64]{1,0:T(8,128)S(1)} %get-tuple-element.9.a, f32[1,64]{1,0:T(1,128)S(1)} %get-tuple-element.10.b, f32[1,48]{1,0:T(1,128)S(1)} %get-tuple-element.11.c), custom_call_target="tpu_custom_call" | custom-call | tf_op jit(solution)/shard_map/pallas_call | solution.py:356
Async XLA Ops:
  0.6 0.7 %copy-start = (s32[64,1]{0,1:T(1,128)S(1)}, s32[64,1]{0,1:T(1,128)}, u32[]{:S(2)}) copy-start(s32[64,1]{0,1:T(1,128)} %param.6) | copy-start | bytes 772
  0.6 0.7 %copy-start.1 = (s32[64,1]{0,1:T(1,128)S(1)}, s32[64,1]{0,1:T(1,128)}, u32[]{:S(2)}) copy-start(s32[64,1]{0,1:T(1,128)} %param.7) | copy-start | bytes 772

commit v7 on v6

--- a/solution.py
+++ b/solution.py
@@ -23,13 +23,14 @@
 BF16 = jnp.bfloat16
 MESH = pl.DeviceIdType.MESH
 AWAY = (4, 3, 5, 2, 6, 1, 7, 0)
+VIA = (None, None, 3, 3, 1, 3, 1, 3)
 
 
 def kernel(
     wave_hbm, temp_hbm, lag_hbm, pres_hbm, score_ref, mad_ref, peak_ref,
-    wave_ref, temp_ref, lag_ref, pres_ref, sem_in, wrow, amat, hank0, hank1, hank2, part, scl, sendc, own, recvc, sendx, recvx, sendz, recvz,
+    wave_ref, temp_ref, lag_ref, pres_ref, sem_in, wrow, amat, hank0, hank1, hank2, part, scl, sendc, own, recvc, sendx, recvx, recvr, sendz, recvz,
     outr, got, pk, pkgot,
-    sem_cs, sem_cr, sem_xs, sem_xr, sem_zs, sem_zr, sem_os, sem_or, sem_ps, sem_pr,
+    sem_cs, sem_cr, sem_xs, sem_xr, sem_rs, sem_rr, sem_zs, sem_zr, sem_os, sem_or, sem_ps, sem_pr,
 ):
     s = lax.axis_index("sta")
     tp = lax.axis_index("tpl")
@@ -134,20 +135,24 @@
     def shifted(t):
         lag = lag_ref[0, t]
         here = pres_ref[0, t].astype(F32)
-        a, r = lag // 128, lag % 128
+        a, r = lax.shift_right_logical(lag, 7), lax.bitwise_and(lag, 127)
         left = right = None
         for q in range(NQ):
             at = (q * NT + t) * NBLK + 2 * q + a
             one, two = part[pl.ds(at, ROWS), :], part[pl.ds(at + 1, ROWS), :]
             left = one if left is None else left + one
             right = two if right is None else right + two
-        by = (128 - r) % 128
+        by = lax.bitwise_and(128 - r, 127)
         left, right = pltpu.roll(left, by, 1), pltpu.roll(right, by, 1)
         return jnp.where(lane24 < 128 - r, left, right) * (scl[pl.ds(t, 1), :] * here)
 
     def place(k):
         return (z + 4 + k // 2 - (k % 2) * k + 8) % 8
 
+    beyond = [(z + AWAY[k]) % 8 for k in range(8)]
+    others = [(x + d) % 4 for d in range(4)]
+    group = [others[d] * 16 for d in range(4)]
+
     def copy_c(k):
         return pltpu.make_async_remote_copy(
             src_ref=sendc.at[k], dst_ref=recvc.at[k], send_sem=sem_cs.at[k], recv_sem=sem_cr.at[k],
@@ -157,45 +162,65 @@
         return pltpu.make_async_remote_copy(
             src_ref=sendx.at[k, d - 1], dst_ref=recvx.at[k, d - 1],
             send_sem=sem_xs.at[k, d - 1], recv_sem=sem_xr.at[k, d - 1],
-            device_id=dev((x + d) % 4, z, c), device_id_type=MESH)
+            device_id=dev(others[d], z, c), device_id_type=MESH)
+
+    def copy_r(k):
+        return pltpu.make_async_remote_copy(
+            src_ref=sendx.at[k, 1], dst_ref=recvr.at[k], send_sem=sem_rs.at[k],
+            recv_sem=sem_rr.at[k], device_id=dev(others[VIA[k]], z, c), device_id_type=MESH)
 
     def copy_z(k):
         return pltpu.make_async_remote_copy(
             src_ref=sendz.at[k], dst_ref=recvz.at[k], send_sem=sem_zs.at[k], recv_sem=sem_zr.at[k],
-            device_id=dev(x, (z + AWAY[k]) % 8, c), device_id_type=MESH)
-
-    def both(k, _):
+            device_id=dev(x, beyond[k], c), device_id_type=MESH)
+
+    def both(k):
+        at = beyond[k] * 2
         for d in range(4):
-            sendc[k, d] = shifted(((x + d) % 4) * 16 + place(k) * 2 + 1 - c)
+            sendc[k, d] = shifted(group[d] + at + 1 - c)
         copy_c(k).start()
         for d in range(4):
-            own[k, d] = shifted(((x + d) % 4) * 16 + place(k) * 2 + c)
-        return 0
-
-    def fold(k, _):
+            own[k, d] = shifted(group[d] + at + c)
+
+    def fold(k):
         copy_c(k).wait_recv()
         for d in (2, 1, 3):
-            sendx[k, d - 1] = own[k, d] + recvc[k, d]
-            copy_x(k, d).start()
-        return 0
-
-    def both_fold(k, _):
-        both(k, 0)
-        fold(k - 5, 0)
-        return 0
+            if d != VIA[k]:
+                sendx[k, d - 1] = own[k, d] + recvc[k, d]
+                (copy_r(k) if d == 2 and VIA[k] else copy_x(k, d)).start()
+
+    def relay(k):
+        copy_r(k).wait_recv()
+        d = VIA[k]
+        sendx[k, d - 1] = (own[k, d] + recvc[k, d]) + recvr[k]
+        copy_x(k, d).start()
+
+    def reduced(k):
+        total = own[k, 0] + recvc[k, 0]
+        for d in (1, 3) if VIA[k] else (1, 3, 2):
+            copy_x(k, d).wait_recv()
+            total = total + recvx[k, d - 1]
+        if k < 7:
+            sendz[k] = total
+            copy_z(k).start()
+        return total
 
     pl.semaphore_wait(barrier, 1 + 3 + 7 + 7)
-    lax.fori_loop(0, 5, both, 0)
-    lax.fori_loop(5, 8, both_fold, 0)
-    lax.fori_loop(3, 8, fold, 0)
-    row = None
     for k in range(8):
-        for d in (1, 3, 2):
-            copy_x(k, d).wait_recv()
-        row = (own[k, 0] + recvc[k, 0]) + (recvx[k, 0] + recvx[k, 1] + recvx[k, 2])
-        if k < 7:
-            sendz[k] = row
-            copy_z(k).start()
+        both(k)
+        if k >= 5:
+            fold(k - 5)
+    for k in range(3, 8):
+        fold(k)
+    relay(2)
+    reduced(0)
+    relay(3)
+    reduced(1)
+    for k in range(4, 8):
+        relay(k)
+    for k in range(2, 7):
+        reduced(k)
+    row = reduced(7)
     for k in range(7):
         copy_z(k).wait_recv()
         row = row + recvz[k]
@@ -253,8 +278,6 @@
             src_ref=outr.at[to], dst_ref=got.at[s], send_sem=sem_os, recv_sem=sem_or,
             device_id=(to, tp), device_id_type=MESH)
 
-    others = [(x + d) % 4 for d in range(4)]
-
     def send(k, _):
         zz = place(k)
         for d in (2, 1, 3, 0):
@@ -292,7 +315,7 @@
     for k in range(8):
         copy_c(k).wait_send()
         for d in range(1, 4):
-            copy_x(k, d).wait_send()
+            (copy_r(k) if d == 2 and VIA[k] else copy_x(k, d)).wait_send()
     for k in range(7):
         copy_z(k).wait_send()
         copy_p(k + 1).wait_send()
@@ -341,13 +364,15 @@
             pltpu.VMEM((8, 4, ROWS, 128), F32),
             pltpu.VMEM((8, 3, ROWS, 128), F32),
             pltpu.VMEM((8, 3, ROWS, 128), F32),
+            pltpu.VMEM((8, ROWS, 128), F32),
             pltpu.VMEM((7, ROWS, 128), F32),
             pltpu.VMEM((7, ROWS, 128), F32),
             pltpu.VMEM((64, 1, 128), F32),
             pltpu.VMEM((64, 1, 128), F32),
             pltpu.VMEM((ROWS, 128), F32),
             pltpu.VMEM((8, 1, 128), F32),
-            dma((8,)), dma((8,)), dma((8, 3)), dma((8, 3)), dma((7,)), dma((7,)),
+            dma((8,)), dma((8,)), dma((8, 3)), dma((8, 3)), dma((8,)), dma((8,)),
+            dma((7,)), dma((7,)),
             dma(()), dma(()), dma((7,)), dma((7,)),
         ],
         compiler_params=pltpu.CompilerParams(

time: 39.9 us -> 41.7 us (1.045)
  Pallas kernels: 38.5 us -> 40.3 us
    pallas_call x1, Pallas kernels: 37.8 us -> 39.6 us  [on_device(): pl.pallas_call(kernel, out_shape=(jax.ShapeDtypeStruct((OWN, NT), F32), j...]
where the time goes in v7:
time: 41.7 us; the launch traced here: 41.6 us
  Pallas kernels  40.3 us (97%)
  local copies, waits for them, and re-layouts  0.66 us (2%)
  between operations  0.66 us (2%)
    pallas_call x1, Pallas kernels, on_device(): pl.pallas_call(kernel, out_shape=(jax.ShapeDtypeStruct((OWN, NT), F32), j...  39.6 us

profile of v7, /device:TPU:1, one launch (start us, length us, event | category | flops | bytes accessed | tf_op | source)
XLA Modules:
  0.0 41.6 jit_solution(1465158651911956568)
XLA Ops:
  0.6 0.0 copy-start
  0.6 0.0 copy-start.1
  0.7 0.6 %copy-done = s32[64,1]{0,1:T(1,128)S(1)} copy-done((s32[64,1]{0,1:T(1,128)S(1)}, s32[64,1]{0,1:T(1,128)}, u32[]{:S(2)}) %copy-start) | copy-done | bytes 280
  1.3 0.0 copy-done.1
  1.3 39.6 %shard_map.67 = (f32[48,64]{1,0:T(8,128)S(1)}, f32[1,64]{1,0:T(1,128)S(1)}, f32[1,48]{1,0:T(1,128)S(1)}) custom-call(bf16[3,6583]{1,0:T(4,128)(2,1)} %bitcast.9, bf16[64,1536]{1,0:T(8,128)(2,1)} %bitcast.8, s32[1,64]{1,0:T(1,128)S(1)} %bitcast.6, s32[1,64]{1,0:T(1,128)S(1)} %bitcast.7), custom_call_target="tpu_custom_call" | custom-call | tf_op jit(solution)/shard_map/pallas_call | solution.py:340
  41.0 0.6 %shard_map.68 = (f32[48,64]{1,0:T(8,128)}, f32[1,64]{1,0:T(1,128)}, f32[1,48]{1,0:T(1,128)}) custom-call(f32[48,64]{1,0:T(8,128)S(1)} %get-tuple-element.9.a, f32[1,64]{1,0:T(1,128)S(1)} %get-tuple-element.10.b, f32[1,48]{1,0:T(1,128)S(1)} %get-tuple-element.11.c), custom_call_target="tpu_custom_call" | custom-call | tf_op jit(solution)/shard_map/pallas_call | solution.py:381
Async XLA Ops:
  0.6 0.7 %copy-start = (s32[64,1]{0,1:T(1,128)S(1)}, s32[64,1]{0,1:T(1,128)}, u32[]{:S(2)}) copy-start(s32[64,1]{0,1:T(1,128)} %param.6) | copy-start | bytes 772
  0.6 0.7 %copy-start.1 = (s32[64,1]{0,1:T(1,128)S(1)}, s32[64,1]{0,1:T(1,128)}, u32[]{:S(2)}) copy-start(s32[64,1]{0,1:T(1,128)} %param.7) | copy-start | bytes 772

commit v8 on v7

--- a/solution.py
+++ b/solution.py
@@ -23,14 +23,13 @@
 BF16 = jnp.bfloat16
 MESH = pl.DeviceIdType.MESH
 AWAY = (4, 3, 5, 2, 6, 1, 7, 0)
-VIA = (None, None, 3, 3, 1, 3, 1, 3)
 
 
 def kernel(
     wave_hbm, temp_hbm, lag_hbm, pres_hbm, score_ref, mad_ref, peak_ref,
-    wave_ref, temp_ref, lag_ref, pres_ref, sem_in, wrow, amat, hank0, hank1, hank2, part, scl, sendc, own, recvc, sendx, recvx, recvr, sendz, recvz,
+    wave_ref, temp_ref, lag_ref, pres_ref, sem_in, wrow, amat, hank0, hank1, hank2, part, scl, sendc, own, recvc, sendx, recvx, sendz, recvz,
     outr, got, pk, pkgot,
-    sem_cs, sem_cr, sem_xs, sem_xr, sem_rs, sem_rr, sem_zs, sem_zr, sem_os, sem_or, sem_ps, sem_pr,
+    sem_cs, sem_cr, sem_xs, sem_xr, sem_zs, sem_zr, sem_os, sem_or, sem_ps, sem_pr,
 ):
     s = lax.axis_index("sta")
     tp = lax.axis_index("tpl")
@@ -57,24 +56,8 @@
     pl.semaphore_signal(barrier, inc=1, device_id=dev(x, z, 1 - c), device_id_type=MESH)
 
     wrow[...] = jnp.zeros(wrow.shape, F32)
-    for copy in inputs:
-        copy.wait()
+    inputs[1].wait()
     wrow[0:CHANS, 0:SAMPLES] = wave_ref[...].astype(F32)
-
-    total = jnp.zeros((NT, 128), F32)
-    flip_i = lax.broadcasted_iota(jnp.int32, (128, 128), 0)
-    flip_j = lax.broadcasted_iota(jnp.int32, (128, 128), 1)
-    flip = jnp.where(flip_i + flip_j == 127, 1.0, 0.0).astype(BF16)
-    for ch in range(CHANS):
-        for k in range(LEN // TAPS):
-            piece = temp_ref[:, ch * LEN + k * TAPS : ch * LEN + (k + 1) * TAPS]
-            wide = piece.astype(F32)
-            total = total + wide * wide
-            turned = jnp.dot(piece, flip, preferred_element_type=F32).astype(BF16)
-            at = (ch * 2 + k % 2) * TAPS
-            amat[(k // 2) * NT : (k // 2 + 1) * NT, at : at + TAPS] = turned
-    norm = jnp.sqrt(jnp.sum(total, axis=1, keepdims=True) + 1e-6)
-    scl[...] = jnp.broadcast_to(1.0 / norm, (NT, 128))
 
     rho = lax.broadcasted_iota(jnp.int32, (16, 128), 0)
     lane16 = lax.broadcasted_iota(jnp.int32, (16, 128), 1)
@@ -122,6 +105,24 @@
 
     build(0, hank0)
     build(1, hank1, hank0)
+    inputs[0].wait()
+    inputs[2].wait()
+    inputs[3].wait()
+
+    total = jnp.zeros((NT, 128), F32)
+    flip_i = lax.broadcasted_iota(jnp.int32, (128, 128), 0)
+    flip_j = lax.broadcasted_iota(jnp.int32, (128, 128), 1)
+    flip = jnp.where(flip_i + flip_j == 127, 1.0, 0.0).astype(BF16)
+    for ch in range(CHANS):
+        for k in range(LEN // TAPS):
+            piece = temp_ref[:, ch * LEN + k * TAPS : ch * LEN + (k + 1) * TAPS]
+            wide = piece.astype(F32)
+            total = total + wide * wide
+            turned = jnp.dot(piece, flip, preferred_element_type=F32).astype(BF16)
+            at = (ch * 2 + k % 2) * TAPS
+            amat[(k // 2) * NT : (k // 2 + 1) * NT, at : at + TAPS] = turned
+    norm = jnp.sqrt(jnp.sum(total, axis=1, keepdims=True) + 1e-6)
+    scl[...] = jnp.broadcast_to(1.0 / norm, (NT, 128))
     lax.fori_loop(0, 3, chunks, 0)
     multiply(9, hank0)
     build(11, hank2, hank1)
@@ -164,11 +165,6 @@
             send_sem=sem_xs.at[k, d - 1], recv_sem=sem_xr.at[k, d - 1],
             device_id=dev(others[d], z, c), device_id_type=MESH)
 
-    def copy_r(k):
-        return pltpu.make_async_remote_copy(
-            src_ref=sendx.at[k, 1], dst_ref=recvr.at[k], send_sem=sem_rs.at[k],
-            recv_sem=sem_rr.at[k], device_id=dev(others[VIA[k]], z, c), device_id_type=MESH)
-
     def copy_z(k):
         return pltpu.make_async_remote_copy(
             src_ref=sendz.at[k], dst_ref=recvz.at[k], send_sem=sem_zs.at[k], recv_sem=sem_zr.at[k],
@@ -185,19 +181,12 @@
     def fold(k):
         copy_c(k).wait_recv()
         for d in (2, 1, 3):
-            if d != VIA[k]:
-                sendx[k, d - 1] = own[k, d] + recvc[k, d]
-                (copy_r(k) if d == 2 and VIA[k] else copy_x(k, d)).start()
-
-    def relay(k):
-        copy_r(k).wait_recv()
-        d = VIA[k]
-        sendx[k, d - 1] = (own[k, d] + recvc[k, d]) + recvr[k]
-        copy_x(k, d).start()
+            sendx[k, d - 1] = own[k, d] + recvc[k, d]
+            copy_x(k, d).start()
 
     def reduced(k):
         total = own[k, 0] + recvc[k, 0]
-        for d in (1, 3) if VIA[k] else (1, 3, 2):
+        for d in (1, 3, 2):
             copy_x(k, d).wait_recv()
             total = total + recvx[k, d - 1]
         if k < 7:
@@ -212,13 +201,7 @@
             fold(k - 5)
     for k in range(3, 8):
         fold(k)
-    relay(2)
-    reduced(0)
-    relay(3)
-    reduced(1)
-    for k in range(4, 8):
-        relay(k)
-    for k in range(2, 7):
+    for k in range(7):
         reduced(k)
     row = reduced(7)
     for k in range(7):
@@ -315,7 +298,7 @@
     for k in range(8):
         copy_c(k).wait_send()
         for d in range(1, 4):
-            (copy_r(k) if d == 2 and VIA[k] else copy_x(k, d)).wait_send()
+            copy_x(k, d).wait_send()
     for k in range(7):
         copy_z(k).wait_send()
         copy_p(k + 1).wait_send()
@@ -364,20 +347,24 @@
             pltpu.VMEM((8, 4, ROWS, 128), F32),
             pltpu.VMEM((8, 3, ROWS, 128), F32),
             pltpu.VMEM((8, 3, ROWS, 128), F32),
-            pltpu.VMEM((8, ROWS, 128), F32),
             pltpu.VMEM((7, ROWS, 128), F32),
             pltpu.VMEM((7, ROWS, 128), F32),
             pltpu.VMEM((64, 1, 128), F32),
             pltpu.VMEM((64, 1, 128), F32),
             pltpu.VMEM((ROWS, 128), F32),
             pltpu.VMEM((8, 1, 128), F32),
-            dma((8,)), dma((8,)), dma((8, 3)), dma((8, 3)), dma((8,)), dma((8,)),
-            dma((7,)), dma((7,)),
+            dma((8,)), dma((8,)), dma((8, 3)), dma((8, 3)), dma((7,)), dma((7,)),
             dma(()), dma(()), dma((7,)), dma((7,)),
         ],
         compiler_params=pltpu.CompilerParams(
-            collective_id=0, has_side_effects=True, vmem_limit_bytes=56500000),
-    )(waveform[0], templates[:, 0, :], lags.reshape(1, NT), present.reshape(1, NT))
+            collective_id=0, has_side_effects=True, vmem_limit_bytes=50 * 1024 * 1024),
+    )(
+        *(
+            pltpu.with_memory_space_constraint(value, pltpu.HBM)
+            for value in (
+                waveform[0], templates[:, 0, :], lags.reshape(1, NT), present.reshape(1, NT))
+        )
+    )
     score, mad, peak = pl.pallas_call(
         put_out,
         out_shape=(

time: 41.7 us -> 38.9 us (0.933)
  Pallas kernels: 40.3 us -> 38.1 us
  local copies, waits for them, and re-layouts: 0.66 us -> 0 us
    pallas_call x1, Pallas kernels: 39.6 us -> 37.5 us  [on_device(): pl.pallas_call(kernel, out_shape=(jax.ShapeDtypeStruct((OWN, NT), F32), j...]
    unnamed x4 -> x0, local copies, waits for them, and re-layouts: 0.66 us -> none
where the time goes in v8:
time: 38.9 us; the launch traced here: 38.7 us
  Pallas kernels  38.1 us (98%)
  between operations  0.64 us (2%)
    pallas_call x1, Pallas kernels, on_device(): pl.pallas_call(kernel, out_shape=(jax.ShapeDtypeStruct((OWN, NT), F32), j...  37.5 us

profile of v8, /device:TPU:1, one launch (start us, length us, event | category | flops | bytes accessed | tf_op | source)
XLA Modules:
  0.0 38.7 jit_solution(1668979889978553316)
XLA Ops:
  0.6 37.5 %shard_map.67 = (f32[48,64]{1,0:T(8,128)S(1)}, f32[1,64]{1,0:T(1,128)S(1)}, f32[1,48]{1,0:T(1,128)S(1)}) custom-call(bf16[3,6583]{1,0:T(4,128)(2,1)} %bitcast.7, bf16[64,1536]{1,0:T(8,128)(2,1)} %bitcast.6, s32[1,64]{1,0:T(1,128)} %bitcast.8, s32[1,64]{1,0:T(1,128)} %bitcast.9), custom_call_target="tpu_custom_call" | custom-call | tf_op jit(solution)/shard_map/pallas_call | solution.py:323
  38.1 0.6 %shard_map.68 = (f32[48,64]{1,0:T(8,128)}, f32[1,64]{1,0:T(1,128)}, f32[1,48]{1,0:T(1,128)}) custom-call(f32[48,64]{1,0:T(8,128)S(1)} %get-tuple-element.9.a, f32[1,64]{1,0:T(1,128)S(1)} %get-tuple-element.10.b, f32[1,48]{1,0:T(1,128)S(1)} %get-tuple-element.11.c), custom_call_target="tpu_custom_call" | custom-call | tf_op jit(solution)/shard_map/pallas_call | solution.py:368

commit v9 on v8

--- a/solution.py
+++ b/solution.py
@@ -28,7 +28,7 @@
 def kernel(
     wave_hbm, temp_hbm, lag_hbm, pres_hbm, score_ref, mad_ref, peak_ref,
     wave_ref, temp_ref, lag_ref, pres_ref, sem_in, wrow, amat, hank0, hank1, hank2, part, scl, sendc, own, recvc, sendx, recvx, sendz, recvz,
-    outr, got, pk, pkgot,
+    outr, got, pk, pk1, pkgot,
     sem_cs, sem_cr, sem_xs, sem_xr, sem_zs, sem_zr, sem_os, sem_or, sem_ps, sem_pr,
 ):
     s = lax.axis_index("sta")
@@ -48,10 +48,10 @@
         copy.start()
 
     barrier = pltpu.get_barrier_semaphore()
-    for i in range(1, 8):
+    for i in (4, 3, 5, 2, 6, 1, 7):
         pl.semaphore_signal(barrier, inc=1, device_id=(s, (tp + i) % 8), device_id_type=MESH)
         pl.semaphore_signal(barrier, inc=1, device_id=dev(x, (z + i) % 8, c), device_id_type=MESH)
-    for i in range(1, 4):
+    for i in (2, 1, 3):
         pl.semaphore_signal(barrier, inc=1, device_id=dev((x + i) % 4, z, c), device_id_type=MESH)
     pl.semaphore_signal(barrier, inc=1, device_id=dev(x, z, 1 - c), device_id_type=MESH)
 
@@ -156,18 +156,18 @@
 
     def copy_c(k):
         return pltpu.make_async_remote_copy(
-            src_ref=sendc.at[k], dst_ref=recvc.at[k], send_sem=sem_cs.at[k], recv_sem=sem_cr.at[k],
+            src_ref=sendc.at[k], dst_ref=recvc.at[k], send_sem=sem_cs, recv_sem=sem_cr.at[k],
             device_id=dev(x, z, 1 - c), device_id_type=MESH)
 
     def copy_x(k, d):
         return pltpu.make_async_remote_copy(
             src_ref=sendx.at[k, d - 1], dst_ref=recvx.at[k, d - 1],
-            send_sem=sem_xs.at[k, d - 1], recv_sem=sem_xr.at[k, d - 1],
+            send_sem=sem_xs, recv_sem=sem_xr.at[k],
             device_id=dev(others[d], z, c), device_id_type=MESH)
 
     def copy_z(k):
         return pltpu.make_async_remote_copy(
-            src_ref=sendz.at[k], dst_ref=recvz.at[k], send_sem=sem_zs.at[k], recv_sem=sem_zr.at[k],
+            src_ref=sendz.at[k], dst_ref=recvz.at[k], send_sem=sem_zs, recv_sem=sem_zr,
             device_id=dev(x, beyond[k], c), device_id_type=MESH)
 
     def both(k):
@@ -185,10 +185,8 @@
             copy_x(k, d).start()
 
     def reduced(k):
-        total = own[k, 0] + recvc[k, 0]
-        for d in (1, 3, 2):
-            copy_x(k, d).wait_recv()
-            total = total + recvx[k, d - 1]
+        pltpu.make_async_copy(sendx.at[k], recvx.at[k], sem_xr.at[k]).wait()
+        total = (own[k, 0] + recvc[k, 0]) + (recvx[k, 0] + recvx[k, 1] + recvx[k, 2])
         if k < 7:
             sendz[k] = total
             copy_z(k).start()
@@ -204,8 +202,8 @@
     for k in range(7):
         reduced(k)
     row = reduced(7)
+    pltpu.make_async_copy(sendz, recvz, sem_zr).wait()
     for k in range(7):
-        copy_z(k).wait_recv()
         row = row + recvz[k]
 
     pos = jnp.clip(jnp.abs(row) * (BINS / 512.0) - 0.5, 0.0, BINS - 1.0)
@@ -229,15 +227,18 @@
     over = jnp.concatenate([jnp.zeros((1, 1), F32), counts[32:33, 0:31]], axis=1)
     row_l = lax.broadcasted_iota(jnp.int32, (32, 32), 0)
     col_h = lax.broadcasted_iota(jnp.int32, (32, 32), 1)
-    counts = counts[0:32, :] + jnp.where(row_l == 0, jnp.broadcast_to(over, (32, 32)), 0.0)
     below = jnp.where(col_h < row_l, 1.0, 0.0)
     above = jnp.where(row_l < col_h, 1.0, 0.0)
     sums = jnp.broadcast_to(jnp.sum(counts, axis=0, keepdims=True), (8, 32))
-    before = jnp.dot(below, counts, precision=lax.Precision.HIGHEST, preferred_element_type=F32)
+    before = jnp.dot(
+        below, counts[0:32, :], precision=lax.Precision.HIGHEST, preferred_element_type=F32)
     before = before + jnp.dot(
         sums, above, precision=lax.Precision.HIGHEST, preferred_element_type=F32)[0:1, :]
+    over = jnp.where(row_l == 0, jnp.broadcast_to(over, (32, 32)), 0.0)
+    before = before - over
+    counts = counts[0:32, :] + over
     share = jnp.clip((0.5 * TOUT - before) / jnp.maximum(counts, 1.0), 0.0, 1.0)
-    share = jnp.sum(jnp.sum(share, axis=1, keepdims=True), axis=0, keepdims=True)
+    share = jnp.sum(jnp.sum(share, axis=0, keepdims=True), axis=1, keepdims=True)
     mad = 1.4826 * ((512.0 / BINS) * share)
     pk[...] = row / mad
     madrow = jnp.broadcast_to(mad, (8, 128))
@@ -277,12 +278,11 @@
     pltpu.make_async_copy(outr.at[pl.ds(0, 63)], got.at[pl.ds(0, 63)], sem_or).wait()
 
     best = jnp.max(got[...], axis=0)
-    pkgot[0] = best
+    pk1[...] = best
 
     def copy_p(d):
         return pltpu.make_async_remote_copy(
-            src_ref=pkgot.at[0], dst_ref=pkgot.at[d], send_sem=sem_ps.at[d - 1],
-            recv_sem=sem_pr.at[d - 1], device_id=(s, (tp + d) % 8), device_id_type=MESH)
+            src_ref=pk1, dst_ref=pkgot.at[d - 1], send_sem=sem_ps, recv_sem=sem_pr, device_id=(s, (tp + d) % 8), device_id_type=MESH)
 
     for d in (4, 3, 5, 2, 6, 1, 7):
         copy_p(d).start()
@@ -290,18 +290,15 @@
     turned = flat.T
     score_ref[...] = turned[0:OWN, 0:NT]
     mad_ref[...] = turned[OWN : OWN + 1, 0:NT]
-    for d in (1, 7, 2, 6, 3, 5, 4):
-        copy_p(d).wait_recv()
+    pltpu.make_async_copy(pkgot, pkgot, sem_pr).wait()
+    for d in range(7):
         best = jnp.maximum(best, pkgot[d])
     peak_ref[...] = best[:, 0:OWN]
 
-    for k in range(8):
-        copy_c(k).wait_send()
-        for d in range(1, 4):
-            copy_x(k, d).wait_send()
-    for k in range(7):
-        copy_z(k).wait_send()
-        copy_p(k + 1).wait_send()
+    pltpu.make_async_copy(sendc, recvc, sem_cs).wait()
+    pltpu.make_async_copy(sendx, recvx, sem_xs).wait()
+    pltpu.make_async_copy(sendz, recvz, sem_zs).wait()
+    pltpu.make_async_copy(pkgot, pkgot, sem_ps).wait()
     pltpu.make_async_copy(outr.at[pl.ds(0, 63)], got.at[pl.ds(0, 63)], sem_os).wait()
 
 
@@ -352,9 +349,10 @@
             pltpu.VMEM((64, 1, 128), F32),
             pltpu.VMEM((64, 1, 128), F32),
             pltpu.VMEM((ROWS, 128), F32),
-            pltpu.VMEM((8, 1, 128), F32),
-            dma((8,)), dma((8,)), dma((8, 3)), dma((8, 3)), dma((7,)), dma((7,)),
-            dma(()), dma(()), dma((7,)), dma((7,)),
+            pltpu.VMEM((1, 128), F32),
+            pltpu.VMEM((7, 1, 128), F32),
+            dma(()), dma((8,)), dma(()), dma((8,)), dma(()), dma(()),
+            dma(()), dma(()), dma(()), dma(()),
         ],
         compiler_params=pltpu.CompilerParams(
             collective_id=0, has_side_effects=True, vmem_limit_bytes=50 * 1024 * 1024),

time: 38.9 us -> 38.1 us (0.979)
  Pallas kernels: 38.1 us -> 37.3 us
    pallas_call x1, Pallas kernels: 37.5 us -> 36.7 us  [on_device(): pl.pallas_call(kernel, out_shape=(jax.ShapeDtypeStruct((OWN, NT), F32), j...]
where the time goes in v9:
time: 38.1 us; the launch traced here: 37.9 us
  Pallas kernels  37.3 us (98%)
  between operations  0.64 us (2%)
    pallas_call x1, Pallas kernels, on_device(): pl.pallas_call(kernel, out_shape=(jax.ShapeDtypeStruct((OWN, NT), F32), j...  36.7 us

profile of v9, /device:TPU:1, one launch (start us, length us, event | category | flops | bytes accessed | tf_op | source)
XLA Modules:
  0.0 37.9 jit_solution(12574863058858500882)
XLA Ops:
  0.6 36.7 %shard_map.67 = (f32[48,64]{1,0:T(8,128)S(1)}, f32[1,64]{1,0:T(1,128)S(1)}, f32[1,48]{1,0:T(1,128)S(1)}) custom-call(bf16[3,6583]{1,0:T(4,128)(2,1)} %bitcast.7, bf16[64,1536]{1,0:T(8,128)(2,1)} %bitcast.6, s32[1,64]{1,0:T(1,128)} %bitcast.8, s32[1,64]{1,0:T(1,128)} %bitcast.9), custom_call_target="tpu_custom_call" | custom-call | tf_op jit(solution)/shard_map/pallas_call | solution.py:320
  37.3 0.6 %shard_map.68 = (f32[48,64]{1,0:T(8,128)}, f32[1,64]{1,0:T(1,128)}, f32[1,48]{1,0:T(1,128)}) custom-call(f32[48,64]{1,0:T(8,128)S(1)} %get-tuple-element.9.a, f32[1,64]{1,0:T(1,128)S(1)} %get-tuple-element.10.b, f32[1,48]{1,0:T(1,128)S(1)} %get-tuple-element.11.c), custom_call_target="tpu_custom_call" | custom-call | tf_op jit(solution)/shard_map/pallas_call | solution.py:366

commit v10 on v9

--- a/solution.py
+++ b/solution.py
@@ -27,7 +27,7 @@
 
 def kernel(
     wave_hbm, temp_hbm, lag_hbm, pres_hbm, score_ref, mad_ref, peak_ref,
-    wave_ref, temp_ref, lag_ref, pres_ref, sem_in, wrow, amat, hank0, hank1, hank2, part, scl, sendc, own, recvc, sendx, recvx, sendz, recvz,
+    wave_ref, temp_ref, lag_ref, pres_ref, sem_in, wrow, amat, hank0, hank1, hank2, last0, last1, last2, part, scl, sendc, own, recvc, sendx, recvx, sendz, recvz,
     outr, got, pk, pk1, pkgot,
     sem_cs, sem_cr, sem_xs, sem_xr, sem_zs, sem_zr, sem_os, sem_or, sem_ps, sem_pr,
 ):
@@ -62,13 +62,13 @@
     rho = lax.broadcasted_iota(jnp.int32, (16, 128), 0)
     lane16 = lax.broadcasted_iota(jnp.int32, (16, 128), 1)
 
-    def build(j, into, ahead=None):
+    def build(j, into, ahead=None, old=None, new=None):
         for ch in range(CHANS):
             for g in range(TAPS // 16):
                 rows = slice(ch * TAPS + g * 16, ch * TAPS + (g + 1) * 16)
                 first = lane16 <= rho + 16 * g
-                before = None
-                for b in range(CH + 1):
+                before = None if old is None else old[rows, :].astype(F32)
+                for b in range(0 if old is None else 1, CH + 1):
                     at = pl.multiple_of((j * CH + b) * 128, 128)
                     row = jnp.broadcast_to(wrow[ch : ch + 1, pl.ds(at, 128)], (16, 128))
                     after = pltpu.roll(row, 1 + 16 * g, 1, stride=1, stride_axis=0)
@@ -78,6 +78,8 @@
                         if b == 1 and ahead is not None:
                             ahead[rows, CH * 128 : (CH + 1) * 128] = block
                     before = after
+                if new is not None:
+                    new[rows, :] = before.astype(BF16)
 
     def multiply(j, held, tiles=CH // 2):
         for p in range(tiles):
@@ -96,15 +98,15 @@
 
     def chunks(i, _):
         multiply(3 * i, hank0)
-        build(3 * i + 2, hank2, hank1)
+        build(3 * i + 2, hank2, hank1, last1, last2)
         multiply(3 * i + 1, hank1)
-        build(3 * i + 3, hank0, hank2)
+        build(3 * i + 3, hank0, hank2, last2, last0)
         multiply(3 * i + 2, hank2)
-        build(3 * i + 4, hank1, hank0)
+        build(3 * i + 4, hank1, hank0, last0, last1)
         return 0
 
-    build(0, hank0)
-    build(1, hank1, hank0)
+    build(0, hank0, None, None, last0)
+    build(1, hank1, hank0, last0, last1)
     inputs[0].wait()
     inputs[2].wait()
     inputs[3].wait()
@@ -125,9 +127,9 @@
     scl[...] = jnp.broadcast_to(1.0 / norm, (NT, 128))
     lax.fori_loop(0, 3, chunks, 0)
     multiply(9, hank0)
-    build(11, hank2, hank1)
+    build(11, hank2, hank1, last1, last2)
     multiply(10, hank1)
-    build(12, hank0, hank2)
+    build(12, hank0, hank2, last2)
     multiply(11, hank2)
     multiply(12, hank0, 1)
 
@@ -337,6 +339,9 @@
             pltpu.VMEM((CHANS * TAPS, (CH + 1) * 128), BF16),
             pltpu.VMEM((CHANS * TAPS, (CH + 1) * 128), BF16),
             pltpu.VMEM((CHANS * TAPS, (CH + 1) * 128), BF16),
+            pltpu.VMEM((CHANS * TAPS, 128), BF16),
+            pltpu.VMEM((CHANS * TAPS, 128), BF16),
+            pltpu.VMEM((CHANS * TAPS, 128), BF16),
             pltpu.VMEM((NQ * NT * NBLK, 128), F32),
             pltpu.VMEM((NT, 128), F32),
             pltpu.VMEM((8, 4, ROWS, 128), F32),

time: 38.1 us -> 38 us (level)
  no operation moved by 1% of the time
where the time goes in v10:
time: 38 us; the launch traced here: 37.9 us
  Pallas kernels  37.2 us (98%)
  between operations  0.64 us (2%)
    pallas_call x1, Pallas kernels, on_device(): pl.pallas_call(kernel, out_shape=(jax.ShapeDtypeStruct((OWN, NT), F32), j...  36.6 us

profile of v10, /device:TPU:1, one launch (start us, length us, event | category | flops | bytes accessed | tf_op | source)
XLA Modules:
  0.0 37.9 jit_solution(13627540801861179275)
XLA Ops:
  0.6 36.6 %shard_map.67 = (f32[48,64]{1,0:T(8,128)S(1)}, f32[1,64]{1,0:T(1,128)S(1)}, f32[1,48]{1,0:T(1,128)S(1)}) custom-call(bf16[3,6583]{1,0:T(4,128)(2,1)} %bitcast.7, bf16[64,1536]{1,0:T(8,128)(2,1)} %bitcast.6, s32[1,64]{1,0:T(1,128)} %bitcast.8, s32[1,64]{1,0:T(1,128)} %bitcast.9), custom_call_target="tpu_custom_call" | custom-call | tf_op jit(solution)/shard_map/pallas_call | solution.py:322
  37.2 0.6 %shard_map.68 = (f32[48,64]{1,0:T(8,128)}, f32[1,64]{1,0:T(1,128)}, f32[1,48]{1,0:T(1,128)}) custom-call(f32[48,64]{1,0:T(8,128)S(1)} %get-tuple-element.9.a, f32[1,64]{1,0:T(1,128)S(1)} %get-tuple-element.10.b, f32[1,48]{1,0:T(1,128)S(1)} %get-tuple-element.11.c), custom_call_target="tpu_custom_call" | custom-call | tf_op jit(solution)/shard_map/pallas_call | solution.py:371

commit v11 on v10

--- a/solution.py
+++ b/solution.py
@@ -242,7 +242,7 @@
     share = jnp.clip((0.5 * TOUT - before) / jnp.maximum(counts, 1.0), 0.0, 1.0)
     share = jnp.sum(jnp.sum(share, axis=0, keepdims=True), axis=1, keepdims=True)
     mad = 1.4826 * ((512.0 / BINS) * share)
-    pk[...] = row / mad
+    pk[0:ROWS] = row / mad
     madrow = jnp.broadcast_to(mad, (8, 128))
 
     lane8 = lax.broadcasted_iota(jnp.int32, (8, 128), 1)
@@ -342,7 +342,7 @@
             pltpu.VMEM((CHANS * TAPS, 128), BF16),
             pltpu.VMEM((CHANS * TAPS, 128), BF16),
             pltpu.VMEM((CHANS * TAPS, 128), BF16),
-            pltpu.VMEM((NQ * NT * NBLK, 128), F32),
+            pltpu.VMEM((NQ * NT * NBLK + 64, 128), F32),
             pltpu.VMEM((NT, 128), F32),
             pltpu.VMEM((8, 4, ROWS, 128), F32),
             pltpu.VMEM((8, 4, ROWS, 128), F32),
@@ -353,7 +353,7 @@
             pltpu.VMEM((7, ROWS, 128), F32),
             pltpu.VMEM((64, 1, 128), F32),
             pltpu.VMEM((64, 1, 128), F32),
-            pltpu.VMEM((ROWS, 128), F32),
+            pltpu.VMEM((ROWS + 8, 128), F32),
             pltpu.VMEM((1, 128), F32),
             pltpu.VMEM((7, 1, 128), F32),
             dma(()), dma((8,)), dma(()), dma((8,)), dma(()), dma(()),

time: 38 us -> 38 us (level)
  no operation moved by 1% of the time
where the time goes in v11:
time: 38 us; the launch traced here: 37.9 us
  Pallas kernels  37.2 us (98%)
  between operations  0.64 us (2%)
    pallas_call x1, Pallas kernels, on_device(): pl.pallas_call(kernel, out_shape=(jax.ShapeDtypeStruct((OWN, NT), F32), j...  36.6 us

profile of v11, /device:TPU:1, one launch (start us, length us, event | category | flops | bytes accessed | tf_op | source)
XLA Modules:
  0.0 37.9 jit_solution(530136008948958655)
XLA Ops:
  0.6 36.6 %shard_map.67 = (f32[48,64]{1,0:T(8,128)S(1)}, f32[1,64]{1,0:T(1,128)S(1)}, f32[1,48]{1,0:T(1,128)S(1)}) custom-call(bf16[3,6583]{1,0:T(4,128)(2,1)} %bitcast.7, bf16[64,1536]{1,0:T(8,128)(2,1)} %bitcast.6, s32[1,64]{1,0:T(1,128)} %bitcast.8, s32[1,64]{1,0:T(1,128)} %bitcast.9), custom_call_target="tpu_custom_call" | custom-call | tf_op jit(solution)/shard_map/pallas_call | solution.py:322
  37.2 0.6 %shard_map.68 = (f32[48,64]{1,0:T(8,128)}, f32[1,64]{1,0:T(1,128)}, f32[1,48]{1,0:T(1,128)}) custom-call(f32[48,64]{1,0:T(8,128)S(1)} %get-tuple-element.9.a, f32[1,64]{1,0:T(1,128)S(1)} %get-tuple-element.10.b, f32[1,48]{1,0:T(1,128)S(1)} %get-tuple-element.11.c), custom_call_target="tpu_custom_call" | custom-call | tf_op jit(solution)/shard_map/pallas_call | solution.py:371
